TPU v7x, 512 devices: a whole 4x8x8 slice. The times are simulated.
512 devices in a mesh: pt: 32 (over y_hi, z), orb: 16 (over x, y_lo, core).
Axes of the slice: x: 4, y: 8 (y_hi: 4, y_lo: 2; y = y_hi * 2 + y_lo), z: 8, core: 2. Of those that a mesh axis runs over, the one named last changes fastest.
Arguments:
- panel_cols: int32 [32], replicated, may hold values from 0 to 16383, as said below
- occ_orbitals: bfloat16 [16384, 2048], P('pt', 'orb'), may hold values from -0.890625 to 0.890625
- vir_orbitals: bfloat16 [16384, 8192], P('pt', 'orb'), may hold values from -0.62890625 to 0.62890625
- occ_energy: float32 [2048], P('orb'), may hold values from 0.05 to 2
- vir_energy: float32 [8192], P('orb'), may hold values from 0.05 to 3
- coulomb: float32 [16384, 16384], P('pt', 'orb'), may hold values from -0.046875 to 0.046875
Outputs:
- screened: float32 [16384, 512], P(('orb', 'pt'))
Inputs may be any that keep to these rules, and one draw needn't show every extreme that they name: `panel_cols`: 32 different interpolation point indices.
All inputs are finite; a program needn't handle non-finite values.
Results may differ from a plain program's by a relative error of at most 0.0003.
Values may be sent and summed in bfloat16 or wider, within the bound.
No kernel may reach another device: no remote copies, remote signals or barrier semaphores. Data moves between devices by JAX's collectives and lax.ppermute only.
A program may use at most 64 MiB of HBM per device.

v0:
```python
import jax
import jax.numpy as jnp
from jax import lax
from jax.sharding import Mesh
from jax.sharding import PartitionSpec as P

NT = 16
NF = 16
NC = 32
PT = ("pt_0", "pt_1")
ORB_PT = ("orb", "pt_0", "pt_1")


def sent_to_all(x, axis):
    copies = jnp.broadcast_to(x, (lax.axis_size(axis), *x.shape))
    return lax.all_to_all(copies, axis, split_axis=0, concat_axis=0, tiled=True)


def over_copies(x, axis):
    return sent_to_all(x, axis).astype(jnp.float32).sum(axis=0)


def split_up(x, dim, devices):
    shape = x.shape
    blocks = x.reshape(*shape[:dim], devices, shape[dim] // devices, *shape[dim + 1 :])
    return jnp.moveaxis(blocks, dim, 0)


def sent_and_summed(x, axis, dim):
    blocks = split_up(x, dim, lax.axis_size(axis))
    arrived = lax.all_to_all(blocks, axis, split_axis=0, concat_axis=0, tiled=True)
    return arrived.sum(axis=0)


def sent_together(arrays, axis, dim, along):
    widths = [a.shape[along] for a in arrays]
    both = jnp.concatenate(arrays, axis=along)
    filled = sent_and_summed(both, axis, dim)
    return tuple(jnp.split(filled, [sum(widths[:k]) for k in range(1, len(widths))], axis=along))


def joined_along(blocks, dim):
    shape = list(blocks.shape[1:])
    shape[dim] *= blocks.shape[0]
    return jnp.moveaxis(blocks, 0, dim).reshape(shape)


def collect(x, axis, dim):
    return joined_along(sent_to_all(x, axis), dim)


def own_block(blocks, axes, order):
    shape = [lax.axis_size(a) for a in axes]
    blocks = blocks.reshape(*shape, *blocks.shape[1:])
    blocks = blocks.transpose(*order, *range(len(axes), blocks.ndim))
    blocks = blocks.reshape(-1, *blocks.shape[len(axes) :])
    for k in order:
        blocks = lax.psum_scatter(blocks, axes[k], scatter_dimension=0, tiled=True)
    return blocks[0]


def sum_by_axis_2(x, axes, order, dim):
    devices = lax.axis_size(axes)
    return own_block(split_up(x, dim, devices), axes, order)


def quadrature():
    moments = 0.05 * jnp.exp(0.3 * jnp.arange(NT, dtype=jnp.float32))
    freqs = 0.1 * jnp.exp(0.3 * jnp.arange(NF, dtype=jnp.float32))
    return (moments, 0.3 * moments[None, :] * jnp.cos(freqs[:, None] * moments[None, :]))


def scaled_panel(panel_rows, energy, moments):
    decay = jnp.exp(-energy[:, None] * moments[None, :])
    scaled = panel_rows.T[:, :, None] * decay[:, None, :]
    return scaled.reshape(energy.shape[0], NC * NT).astype(jnp.bfloat16)


def transform(product, cosine_table):
    point_count = product.shape[0]
    shaped = product.reshape(point_count, NC, NT)
    return jnp.einsum("rct,ft->rcf", shaped, cosine_table, precision=lax.Precision.HIGHEST).reshape(
        point_count, NC * NF
    )


def local(panel_cols, occ_orbitals, vir_orbitals, occ_energy, vir_energy, coulomb):
    moments, cosine_table = quadrature()
    local_points = occ_orbitals.shape[0]
    point_base = lax.axis_index(PT) * local_points
    positions = lax.broadcasted_iota(jnp.int32, (panel_cols.shape[0], local_points), 1)
    selector = (panel_cols[:, None] - point_base == positions).astype(jnp.bfloat16)
    occ_pick = jnp.dot(selector, occ_orbitals, preferred_element_type=jnp.float32)
    vir_pick = jnp.dot(selector, vir_orbitals, preferred_element_type=jnp.float32)
    occ_panel, vir_panel = (
        over_copies(occ_pick.astype(jnp.bfloat16), PT).astype(jnp.float32),
        over_copies(vir_pick.astype(jnp.bfloat16), PT).astype(jnp.float32),
    )
    occ_scaled = scaled_panel(occ_panel, occ_energy, moments)
    vir_scaled = scaled_panel(vir_panel, vir_energy, moments)
    occ_partial = jnp.dot(occ_orbitals, occ_scaled, preferred_element_type=jnp.float32)
    vir_partial = jnp.dot(vir_orbitals, vir_scaled, preferred_element_type=jnp.float32)
    green_occ, green_vir = sent_together((occ_partial, vir_partial), "orb", 0, 1)
    polar = collect(transform(green_occ * green_vir, cosine_table), "orb", 0)
    return sum_by_axis_2(
        lax.dot_general(
            coulomb,
            polar,
            (((0,), (0,)), ((), ())),
            precision=lax.Precision.HIGHEST,
            preferred_element_type=jnp.float32,
        ),
        PT,
        (1, 0),
        0,
    )


def solution(mesh):
    finer = Mesh(mesh.devices.reshape(4, 8, mesh.shape["orb"]), ("pt_0", "pt_1", "orb"))
    placed = (P(), P(PT, "orb"), P(PT, "orb"), P("orb"), P("orb"), P(PT, "orb"))
    return jax.shard_map(
        local, mesh=finer, in_specs=placed, out_specs=P(ORB_PT, None), check_vma=False
    )
```

profile of v0, /device:TPU:16, one launch (start us, length us, event | category | flops | bytes accessed | tf_op | source)
XLA Modules:
  0.0 223.5 jit_solution(16139626948577841970)
XLA Ops:
  6.5 0.0 copy-start
  6.5 0.8 broadcast_subtract_fusion
  7.3 1.1 convolution_convert_fusion.1
  8.4 0.7 broadcast_in_dim.6
  9.2 0.0 copy-start.5
  9.2 0.0 copy-start.6
  9.2 16.2 %all-to-all-start = ((bf16[32,32,128]{2,1,0:T(8,128)(2,1)}), bf16[32,32,128]{2,1,0:T(8,128)(2,1)S(1)}, u32[]{:S(2)}, u32[]{:S(2)}) async-start(bf16[32,32,128]{2,1,0:T(8,128)(2,1)} %broadcast_in_dim.6), calls=%async_computation | async-start | bytes 524288 | tf_op jit(solution)/shard_map/all_to_all | solution.py:16
  25.4 0.0 copy-start.3
  25.4 1.3 convolution_convert_fusion
  26.7 12.7 %all-to-all-done = bf16[32,32,128]{2,1,0:T(8,128)(2,1)S(1)} async-done(((bf16[32,32,128]{2,1,0:T(8,128)(2,1)}), bf16[32,32,128]{2,1,0:T(8,128)(2,1)S(1)}, u32[]{:S(2)}, u32[]{:S(2)}) %all-to-all-start) | async-done | bytes 262176 | tf_op jit(solution)/shard_map/all_to_all | solution.py:16
  39.4 1.1 broadcast_in_dim.7
  40.5 5.0 %all-to-all-start.1 = ((bf16[32,32,512]{2,1,0:T(8,128)(2,1)}), bf16[32,32,512]{2,1,0:T(8,128)(2,1)S(1)}, u32[]{:S(2)}, u32[]{:S(2)}) async-start(bf16[32,32,512]{2,1,0:T(8,128)(2,1)} %broadcast_in_dim.7), calls=%async_computation.1 | async-start | bytes 2097152 | tf_op jit(solution)/shard_map/all_to_all | solution.py:16
  45.5 0.0 copy-done.5
  45.5 0.0 copy-done.6
  45.5 0.1 multiply_exponential_fusion.1
  45.6 0.7 multiply_exponential_fusion
  46.4 0.0 copy-start.4
  46.4 0.0 copy-done.3
  46.4 1.3 convolution_bitcast_fusion.2
  47.7 26.4 %all-to-all-done.1 = bf16[32,32,512]{2,1,0:T(8,128)(2,1)S(1)} async-done(((bf16[32,32,512]{2,1,0:T(8,128)(2,1)}), bf16[32,32,512]{2,1,0:T(8,128)(2,1)S(1)}, u32[]{:S(2)}, u32[]{:S(2)}) %all-to-all-start.1) | async-done | bytes 1048608 | tf_op jit(solution)/shard_map/all_to_all | solution.py:16
  74.1 0.0 copy-start.2
  74.1 0.0 copy-start.1
  74.1 0.2 convert_reduce_fusion
  74.3 0.0 copy-done.4
  74.3 0.1 multiply_convert_fusion
  74.4 0.8 copy-done.2
  75.2 0.5 convolution_bitcast_fusion.1
  75.6 0.0 copy-done.1
  75.7 1.5 pad_maximum_fusion
  77.1 2.9 %copy.28 = f32[512,1024]{1,0:T(8,128)} copy(f32[512,1024]{0,1:T(8,128)} %pad_maximum_fusion) | data formatting | bytes 4194304 | tf_op jit(solution)/shard_map/concatenate | solution.py:37
  80.1 4.7 %all-to-all-start.2 = ((f32[16,32,1024]{2,1,0:T(8,128)}), f32[16,32,1024]{2,1,0:T(8,128)}, u32[]{:S(2)}, u32[]{:S(2)}) async-start(f32[16,32,1024]{2,1,0:T(8,128)} %bitcast.31), calls=%async_computation.2 | async-start | bytes 4194304 | tf_op jit(solution)/shard_map/all_to_all | solution.py:31
  84.7 0.0 reduce-scatter.3.cloned.1.call-start
  84.8 27.8 %all-to-all-done.2 = f32[16,32,1024]{2,1,0:T(8,128)} async-done(((f32[16,32,1024]{2,1,0:T(8,128)}), f32[16,32,1024]{2,1,0:T(8,128)}, u32[]{:S(2)}, u32[]{:S(2)}) %all-to-all-start.2) | async-done | bytes 2097184 | tf_op jit(solution)/shard_map/all_to_all | solution.py:31
  112.6 1.7 reduce_sum.29
  114.3 0.1 copy.29
  114.5 0.5 fusion.2
  114.9 0.1 copy.32
  115.0 0.1 broadcast_in_dim.8
  115.2 19.3 %all_to_all.20 = f32[16,32,512]{2,1,0:T(8,128)S(1)} all-to-all(f32[16,32,512]{2,1,0:T(8,128)S(1)} %broadcast_in_dim.8), channel_id=1, replica_groups=mesh['pt_0'=4,'pt_1'=8,'orb'=16] {'orb'}, dimensions={0} | all-to-all | bytes 2097152 | tf_op jit(solution)/shard_map/all_to_all | solution.py:16
  134.5 0.0 copy-done
  134.5 4.9 %convolution_bitcast_fusion = f32[1024,512]{0,1:T(8,128)} fusion(f32[512,512]{1,0:T(8,128)S(1)} %bitcast.34, f32[512,1024]{1,0:T(8,128)S(1)} %copy-done), kind=kOutput, calls=%fused_computation.2 | convolution fusion | flops 3221225472 | bytes 5242880 | tf_op jit(solution)/shard_map/dot_general | solution.py:106
  139.4 2.9 %copy.33 = f32[1024,512]{1,0:T(8,128)} copy(f32[1024,512]{0,1:T(8,128)} %convolution_bitcast_fusion) | data formatting | bytes 4194304 | tf_op jit(solution)/shard_map/dot_general | solution.py:106
  142.3 3.2 %copy.34 = f32[8,4,32,512]{3,2,1,0:T(8,128)} copy(f32[8,4,32,512]{3,2,0,1:T(8,128)} %bitcast.33) | data formatting | bytes 4194304 | tf_op jit(solution)/shard_map/transpose | solution.py:55
  145.5 0.0 reduce-scatter.3.cloned.1.call-update
  145.5 0.0 reduce-scatter.5.cloned.1.call-start
  145.6 41.7 %reduce-scatter.3.cloned.1.call-done = f32[4,32,512]{2,1,0:T(8,128)} async-done(((f32[32,32,512]{2,1,0:T(8,128)}), f32[4,32,512]{2,1,0:T(8,128)}) %reduce-scatter.3.cloned.1.call-update) | async-done | bytes 262160 | tf_op jit(solution)/shard_map/reduce_scatter | solution.py:58
  187.3 0.0 reduce-scatter.5.cloned.1.call-update
  187.3 29.3 %reduce-scatter.5.cloned.1.call-done = f32[1,32,512]{2,1,0:T(8,128)} async-done(((f32[4,32,512]{2,1,0:T(8,128)}), f32[1,32,512]{2,1,0:T(8,128)}) %reduce-scatter.5.cloned.1.call-update) | async-done | bytes 65552 | tf_op jit(solution)/shard_map/reduce_scatter | solution.py:58
  (7 shorter events, 0.1 us)
Async XLA Ops:
  6.5 128.0 %copy-start = (f32[512,1024]{1,0:T(8,128)S(1)}, f32[512,1024]{1,0:T(8,128)}, u32[]{:S(2)}) copy-start(f32[512,1024]{1,0:T(8,128)} %param.11) | copy-start | bytes 6291460
  9.2 36.3 %copy-start.5 = (f32[512]{0:T(512)S(1)}, f32[512]{0:T(512)}, u32[]{:S(2)}) copy-start(f32[512]{0:T(512)} %param.10) | copy-start | bytes 6148
  9.2 36.3 %copy-start.6 = (f32[128]{0:T(128)S(1)}, f32[128]{0:T(128)}, u32[]{:S(2)}) copy-start(f32[128]{0:T(128)} %param.9) | copy-start | bytes 1540
  9.2 30.2 %all-to-all-start = ((bf16[32,32,128]{2,1,0:T(8,128)(2,1)}), bf16[32,32,128]{2,1,0:T(8,128)(2,1)S(1)}, u32[]{:S(2)}, u32[]{:S(2)}) async-start(bf16[32,32,128]{2,1,0:T(8,128)(2,1)} %broadcast_in_dim.6), calls=%async_computation | async-start | bytes 524288 | tf_op jit(solution)/shard_map/all_to_all | solution.py:16
  25.4 21.0 %copy-start.3 = (bf16[512,128]{1,0:T(8,128)(2,1)S(1)}, bf16[512,128]{1,0:T(8,128)(2,1)}, u32[]{:S(2)}) copy-start(bf16[512,128]{1,0:T(8,128)(2,1)} %param.7) | copy-start | bytes 393220
  40.5 33.7 %all-to-all-start.1 = ((bf16[32,32,512]{2,1,0:T(8,128)(2,1)}), bf16[32,32,512]{2,1,0:T(8,128)(2,1)S(1)}, u32[]{:S(2)}, u32[]{:S(2)}) async-start(bf16[32,32,512]{2,1,0:T(8,128)(2,1)} %broadcast_in_dim.7), calls=%async_computation.1 | async-start | bytes 2097152 | tf_op jit(solution)/shard_map/all_to_all | solution.py:16
  46.4 27.9 %copy-start.4 = (f32[512,16]{0,1:T(8,128)S(1)}, f32[512,16]{0,1:T(8,128)}, u32[]{:S(2)}) copy-start(f32[512,16]{0,1:T(8,128)} %multiply_exponential_fusion) | copy-start | bytes 98308
  74.1 1.0 copy-start.2
  74.1 1.5 copy-start.1
  80.1 32.5 %all-to-all-start.2 = ((f32[16,32,1024]{2,1,0:T(8,128)}), f32[16,32,1024]{2,1,0:T(8,128)}, u32[]{:S(2)}, u32[]{:S(2)}) async-start(f32[16,32,1024]{2,1,0:T(8,128)} %bitcast.31), calls=%async_computation.2 | async-start | bytes 4194304 | tf_op jit(solution)/shard_map/all_to_all | solution.py:31
  84.7 102.6 %reduce-scatter.3.cloned.1.call-start = ((), (), s32[]{:S(2)}) async-start(), calls=%async_computation.6 | async-start | bytes 2359296 | tf_op jit(solution)/shard_map/reduce_scatter | solution.py:58
  145.5 71.1 %reduce-scatter.5.cloned.1.call-start = ((), (), s32[]{:S(2)}) async-start(), calls=%async_computation.7 | async-start | bytes 327680 | tf_op jit(solution)/shard_map/reduce_scatter | solution.py:58
Sparse Core Ops, SparseCore 0:
  145.6 41.6 reduce-scatter.2
  190.1 26.4 reduce-scatter.4
where the time goes:
time: 224 us; the launch traced here: 223 us
  waiting for transfers between devices  138 us (62%)
  starting transfers between devices  26 us (12%)
  blocking collectives  19.3 us (9%)
  between operations  13.6 us (6%)
  local copies, waits for them, and re-layouts  12 us (5%)
  matrix products  9.51 us (4%)
  other arithmetic  5.12 us (2%)
    reduce_scatter x2, waiting for transfers between devices, own_block(): blocks = lax.psum_scatter(blocks, axes[k], scatter_dimension=0, tiled=True)  71.1 us
    all_to_all x2, waiting for transfers between devices, sent_to_all(): return lax.all_to_all(copies, axis, split_axis=0, concat_axis=0, tiled=True)  39 us
    all_to_all x1, waiting for transfers between devices, sent_and_summed(): lax.all_to_all(blocks, axis, split_axis=0, concat_axis=0, tiled=True)  27.8 us
    all_to_all x2, starting transfers between devices, sent_to_all(): return lax.all_to_all(copies, axis, split_axis=0, concat_axis=0, tiled=True)  21.2 us
    all_to_all x1, blocking collectives, sent_to_all(): return lax.all_to_all(copies, axis, split_axis=0, concat_axis=0, tiled=True)  19.3 us
    dot_general x1, matrix products, local(): lax.dot_general(coulomb, polar, (((0,), (0,)), ((), ())), precision=lax.P...  4.86 us
    all_to_all x1, starting transfers between devices, sent_and_summed(): lax.all_to_all(blocks, axis, split_axis=0, concat_axis=0, tiled=True)  4.67 us
  transfers between devices with their start and end apart: 5, of which 5 were waited for; matrix products, arithmetic and copies ran while one was open for 2% of the time, Pallas kernels for 0%

commit v1 on v0

v1 whole, which is shorter than its diff:
```python
import jax
import jax.numpy as jnp
import numpy as np
from jax import lax
from jax.sharding import Mesh
from jax.sharding import PartitionSpec as P

NT = 16
NF = 16
NC = 32
RANK = 10
TWICE = 2
WIDTH = 384
SPARE = 127
YZ = ("yh", "z")
ORB = ("x", "yl", "core")
HIGHEST = lax.Precision.HIGHEST
f32, f16, bf16 = jnp.float32, jnp.float16, jnp.bfloat16


def factors():
    moments = 0.05 * np.exp(0.3 * np.arange(NT))
    freqs = 0.1 * np.exp(0.3 * np.arange(NF))
    table = 0.3 * moments[None, :] * np.cos(freqs[:, None] * moments[None, :])
    u = np.linalg.svd(table)[0][:, :RANK]
    rates = np.exp(np.linspace(np.log(0.1), np.log(5.0), 400))
    typical = u.T @ table @ np.exp(-moments[:, None] * rates[None, :])
    turn = np.linalg.eigh(typical @ typical.T)[1][:, ::-1]
    up = u @ turn
    down = up.T @ table
    slots = [*range(TWICE), *range(TWICE), *range(TWICE, RANK)]
    left = np.zeros((NT, NC, len(slots), NC))
    right = np.zeros((len(slots), NC, NC, NF))
    for k, j in enumerate(slots):
        for c in range(NC):
            left[:, c, k, c] = down[j]
            right[k, c, c, :] = up[:, j]
    return (
        left.reshape(NT * NC, WIDTH).astype(np.float32),
        right.reshape(WIDTH, NC * NF).astype(np.float32),
    )


LEFT, RIGHT = factors()


def moved(x, axes):
    return lax.all_to_all(x, axes, split_axis=0, concat_axis=0, tiled=True)


def power_of(x):
    top = jnp.max(jnp.abs(x), axis=-1, keepdims=True)
    return jnp.ceil(jnp.log2(jnp.maximum(top, 1e-30))) - 14.0


def lanes(x):
    return lax.broadcasted_iota(jnp.int32, x.shape, x.ndim - 1)


def packed(x):
    power = power_of(x)
    scaled = x * jnp.exp2(-power)
    lane = lanes(x)
    rest = scaled - lax.reduce_precision(scaled, 5, 10)
    low = (lane >= 64) & (lane < 128)
    return jnp.where(lane == SPARE, power, jnp.where(low, rest, scaled)).astype(f16)


def unpacked(y):
    power = y[..., SPARE : SPARE + 1].astype(f32)
    y = y.astype(f32)
    return jnp.where(lanes(y) == SPARE, 0.0, y) * jnp.exp2(power)


def local(panel_cols, occ_orbitals, vir_orbitals, occ_energy, vir_energy, coulomb):
    moments = 0.05 * jnp.exp(0.3 * jnp.arange(NT, dtype=f32))
    points, no = occ_orbitals.shape
    nv = vir_orbitals.shape[1]
    width = no + nv
    times = NT * NC
    peers = lax.axis_size(ORB)

    base = lax.axis_index(YZ) * points
    positions = lax.broadcasted_iota(jnp.int32, (NC, points), 1)
    selector = (panel_cols[:, None] - base == positions).astype(bf16)
    pick = jnp.concatenate(
        [jnp.dot(selector, o, preferred_element_type=f32).astype(bf16) for o in (occ_orbitals, vir_orbitals)], axis=1
    )
    rows = moved(pick.reshape(NC, width // 128, 128), YZ).astype(f32).sum(axis=0).astype(bf16)
    panel = moved(jnp.broadcast_to(rows, (NC, *rows.shape)), YZ).reshape(NC, width).astype(f32)

    def green(orbitals, energy, panel):
        decay = jnp.exp(-energy[None, :] * moments[:, None])
        scaled = (panel[None] * decay[:, None]).astype(bf16).reshape(times, -1)
        return lax.dot_general(orbitals, scaled, (((1,), (1,)), ((), ())), preferred_element_type=f32)

    occ = green(occ_orbitals, occ_energy, panel[:, :no])
    vir = green(vir_orbitals, vir_energy, panel[:, no:])
    occ_power, vir_power = power_of(occ), power_of(vir)
    lane = lax.broadcasted_iota(jnp.int32, (points, 128), 1)
    sent = jnp.concatenate(
        [
            (occ * jnp.exp2(-occ_power)).astype(f16),
            (vir * jnp.exp2(-vir_power)).astype(f16),
            jnp.where(lane == 0, occ_power, vir_power).astype(f16),
        ],
        axis=1,
    )
    got = moved(sent.reshape(peers, points // peers, -1), ORB)
    occ_power, vir_power = got[..., 2 * times : 2 * times + 1], got[..., 2 * times + 1 : 2 * times + 2]
    occ = (got[..., :times].astype(f32) * jnp.exp2(occ_power.astype(f32))).sum(axis=0)
    vir = (got[..., times : 2 * times].astype(f32) * jnp.exp2(vir_power.astype(f32))).sum(axis=0)
    polar = packed(jnp.dot(occ * vir, LEFT, precision=HIGHEST, preferred_element_type=f32))
    polar = moved(jnp.broadcast_to(polar, (peers, *polar.shape)), ORB)
    polar = unpacked(polar.reshape(points, WIDTH))
    pair = polar[:, :128]
    pair = pair + jnp.roll(pair, 64, axis=1)
    polar = jnp.concatenate([pair, polar[:, 128:]], axis=1)
    part = lax.dot_general(
        coulomb, polar, (((0,), (0,)), ((), ())), precision=lax.Precision.HIGH, preferred_element_type=f32
    )
    blocks = moved(packed(part).reshape(NC, -1, WIDTH), YZ)
    total = unpacked(blocks).sum(axis=0)
    return jnp.dot(total, RIGHT, precision=HIGHEST, preferred_element_type=f32)


def solution(mesh):
    finer = Mesh(mesh.devices.reshape(4, 8, 4, 2, 2), (*YZ, *ORB))
    placed = (P(), P(YZ, ORB), P(YZ, ORB), P(ORB), P(ORB), P(YZ, ORB))
    return jax.shard_map(local, mesh=finer, in_specs=placed, out_specs=P(ORB + YZ, None), check_vma=False)
```

time: 224 us -> 126 us (0.56)
  the two profiles are of different devices: /device:TPU:16 before, /device:TPU:8 now
where the time goes in v1:
time: 126 us
  blocking collectives  41.7 us (33%)
  waiting for transfers between devices  40 us (32%)
  starting transfers between devices  24.7 us (20%)
  other arithmetic  7.03 us (6%)
  matrix products  6.5 us (5%)
  local copies, waits for them, and re-layouts  5.77 us (5%)
    all_to_all x2, blocking collectives, moved(): return lax.all_to_all(x, axes, split_axis=0, concat_axis=0, tiled=True)  41.7 us
    all_to_all x3, waiting for transfers between devices, moved(): return lax.all_to_all(x, axes, split_axis=0, concat_axis=0, tiled=True)  40 us
    all_to_all x3, starting transfers between devices, moved(): return lax.all_to_all(x, axes, split_axis=0, concat_axis=0, tiled=True)  24.7 us
  transfers between devices with their start and end apart: 3, of which 3 were waited for; matrix products, arithmetic and copies ran while one was open for 1% of the time, Pallas kernels for 0%

profile of v1, /device:TPU:8, one launch (start us, length us, event | category | flops | bytes accessed | tf_op | source)
XLA Modules:
  0.0 125.9 jit_solution(4623795783862990725)
XLA Ops:
  0.0 0.0 copy-start
  0.0 0.0 copy-start.1
  0.0 0.8 broadcast_subtract_fusion
  0.8 1.1 convolution_convert_fusion.1
  1.9 1.3 %convolution_convert_fusion = bf16[32,512]{1,0:T(8,128)(2,1)S(1)} fusion(bf16[512,512]{1,0:T(8,128)(2,1)} %param.10, s32[32]{0:T(128)S(1)} %broadcast_subtract_fusion), kind=kOutput, calls=%fused_computation.6 | convolution fusion | flops 16809984 | bytes 557184 | tf_op jit(solution)/shard_map/dot_general | solution.py:87
  3.2 0.7 reshape.165
  3.9 15.1 %all-to-all-start = ((bf16[32,5,128]{2,1,0:T(8,128)(2,1)}), bf16[32,5,128]{2,1,0:T(8,128)(2,1)S(1)}, u32[]{:S(2)}, u32[]{:S(2)}) async-start(bf16[32,5,128]{2,1,0:T(8,128)(2,1)} %reshape.165), calls=%async_computation | async-start | bytes 131072 | tf_op jit(solution)/shard_map/all_to_all | solution.py:48
  19.0 0.7 neg.40
  19.7 0.7 neg.42
  20.3 0.1 multiply_exponential_fusion
  20.4 0.1 multiply_exponential_fusion.1
  20.5 11.0 %all-to-all-done = bf16[32,5,128]{2,1,0:T(8,128)(2,1)S(1)} async-done(((bf16[32,5,128]{2,1,0:T(8,128)(2,1)}), bf16[32,5,128]{2,1,0:T(8,128)(2,1)S(1)}, u32[]{:S(2)}, u32[]{:S(2)}) %all-to-all-start) | async-done | bytes 40992 | tf_op jit(solution)/shard_map/all_to_all | solution.py:48
  31.5 0.6 broadcast_in_dim.61
  32.2 3.9 %all-to-all-start.1 = ((bf16[32,5,128]{2,1,0:T(8,128)(2,1)}), bf16[32,5,128]{2,1,0:T(8,128)(2,1)S(1)}, u32[]{:S(2)}, u32[]{:S(2)}) async-start(bf16[32,5,128]{2,1,0:T(8,128)(2,1)} %broadcast_in_dim.61), calls=%async_computation.1 | async-start | bytes 131072 | tf_op jit(solution)/shard_map/all_to_all | solution.py:48
  36.0 12.3 %all-to-all-done.1 = bf16[32,5,128]{2,1,0:T(8,128)(2,1)S(1)} async-done(((bf16[32,5,128]{2,1,0:T(8,128)(2,1)}), bf16[32,5,128]{2,1,0:T(8,128)(2,1)S(1)}, u32[]{:S(2)}, u32[]{:S(2)}) %all-to-all-start.1) | async-done | bytes 40992 | tf_op jit(solution)/shard_map/all_to_all | solution.py:48
  48.4 0.0 copy-start.4
  48.4 0.1 multiply_convert_fusion.1
  48.5 0.0 copy-done.1
  48.5 0.5 abs_reduce_fusion.1
  49.0 0.3 copy-done.4
  49.3 0.3 abs_reduce_fusion.2
  49.6 0.1 fusion.6
  49.7 0.1 fusion.7
  49.9 0.1 select_convert_fusion
  50.0 0.4 pad_maximum_fusion
  50.3 1.7 %copy.12 = f16[512,1152]{1,0:T(8,128)(2,1)} copy(f16[512,1152]{0,1:T(8,128)(2,1)S(1)} %pad_maximum_fusion) | data formatting | bytes 2359296 | tf_op jit(solution)/shard_map/concatenate | solution.py:101
  52.0 5.8 %all-to-all-start.2 = ((f16[16,32,1152]{2,1,0:T(8,128)(2,1)}), f16[16,32,1152]{2,1,0:T(8,128)(2,1)S(1)}, u32[]{:S(2)}, u32[]{:S(2)}) async-start(f16[16,32,1152]{2,1,0:T(8,128)(2,1)} %bitcast.27), calls=%async_computation.2 | async-start | bytes 2359296 | tf_op jit(solution)/shard_map/all_to_all | solution.py:48
  57.8 16.7 %all-to-all-done.2 = f16[16,32,1152]{2,1,0:T(8,128)(2,1)S(1)} async-done(((f16[16,32,1152]{2,1,0:T(8,128)(2,1)}), f16[16,32,1152]{2,1,0:T(8,128)(2,1)S(1)}, u32[]{:S(2)}, u32[]{:S(2)}) %all-to-all-start.2) | async-done | bytes 1179680 | tf_op jit(solution)/shard_map/all_to_all | solution.py:48
  74.5 0.0 copy-start.3
  74.5 0.3 exponential_reduce_fusion.2
  74.8 0.3 multiply_reduce_fusion.1
  75.1 0.5 copy-done.3
  75.6 0.6 abs_reduce_fusion.3
  76.3 0.1 fusion.11
  76.5 12.1 %all_to_all.25 = f16[16,32,384]{2,1,0:T(8,128)(2,1)S(1)} all-to-all(f16[16,32,384]{2,1,0:T(8,128)(2,1)S(1)} %broadcast_in_dim.65), channel_id=1, replica_groups=mesh['yh'=4,'z'=8,'x'=4,'yl'=2,'core'=2] {'x','yl','core'}, dimensions={0} | all-to-all | bytes 786432 | tf_op jit(solution)/shard_map/all_to_all | solution.py:48
  88.6 0.2 exponential_reduce_fusion.1
  88.8 0.1 select_multiply_fusion
  89.0 0.1 fusion.16
  89.2 0.1 slice_add_fusion
  89.3 0.0 copy-done
  89.3 1.5 %abs_reduce_fusion = (f32[1024]{0:T(1024)S(1)}, f32[384,1024]{1,0:T(8,128)S(1)}) fusion(f32[512,1024]{1,0:T(8,128)S(1)} %copy-done, f32[512,256]{1,0:T(8,128)S(1)} %slice.62, f32[512,128]{1,0:T(8,128)S(1)} %slice_add_fusion), kind=kOutput, calls=%fused_computation.4 | convolution fusion | flops 1208941568 | bytes 4460544 | tf_op jit(solution)/shard_map/dot_general | solution.py:119
  90.9 1.9 %fusion.1 = f16[1024,384]{0,1:T(8,128)(2,1)} fusion(f32[384,1024]{1,0:T(8,128)S(1)} %get-tuple-element.26, f32[1024]{0:T(1024)S(1)} %get-tuple-element.14, f32[1024]{0:T(1024)S(1)} %get-tuple-element.13, pred[384]{0:T(512)(128)(4,1)S(1)} %get-tuple-element.30, pred[384]{0:T(512)(128)(4,1)S(1)} %get-tuple-element.29), kind=kLoop, calls=%fused_computation.2 | loop fusion | flops 2359296 | bytes 2368256 | tf_op jit(solution)/shard_map/convert_element_type | solution.py:66
  92.8 1.8 %copy.13 = f16[1024,384]{1,0:T(8,128)(2,1)S(1)} copy(f16[1024,384]{0,1:T(8,128)(2,1)} %fusion.1) | data formatting | bytes 1572864 | tf_op jit(solution)/shard_map/convert_element_type | solution.py:66
  94.5 0.0 copy-start.2
  94.5 29.5 %all_to_all.26 = f16[32,32,384]{2,1,0:T(8,128)(2,1)S(1)} all-to-all(f16[32,32,384]{2,1,0:T(8,128)(2,1)S(1)} %bitcast.28), channel_id=1, replica_groups=mesh['yh'=4,'z'=8,'x'=4,'yl'=2,'core'=2] {'yh','z'}, dimensions={0} | all-to-all | bytes 1572864 | tf_op jit(solution)/shard_map/all_to_all | solution.py:48
  124.1 0.4 exponential_reduce_fusion
  124.5 0.2 multiply_reduce_fusion
  124.7 0.0 copy-done.2
  124.7 1.2 fusion.17
  (14 shorter events, 0.2 us)
Async XLA Ops:
  0.0 89.3 %copy-start = (f32[512,1024]{1,0:T(8,128)S(1)}, f32[512,1024]{1,0:T(8,128)}, u32[]{:S(2)}) copy-start(f32[512,1024]{1,0:T(8,128)} %param.13) | copy-start | bytes 6291460
  0.0 48.5 %copy-start.1 = (bf16[512,512]{1,0:T(8,128)(2,1)S(1)}, bf16[512,512]{1,0:T(8,128)(2,1)}, u32[]{:S(2)}) copy-start(bf16[512,512]{1,0:T(8,128)(2,1)} %param.10) | copy-start | bytes 1572868
  3.9 27.6 %all-to-all-start = ((bf16[32,5,128]{2,1,0:T(8,128)(2,1)}), bf16[32,5,128]{2,1,0:T(8,128)(2,1)S(1)}, u32[]{:S(2)}, u32[]{:S(2)}) async-start(bf16[32,5,128]{2,1,0:T(8,128)(2,1)} %reshape.165), calls=%async_computation | async-start | bytes 131072 | tf_op jit(solution)/shard_map/all_to_all | solution.py:48
  32.2 16.2 %all-to-all-start.1 = ((bf16[32,5,128]{2,1,0:T(8,128)(2,1)}), bf16[32,5,128]{2,1,0:T(8,128)(2,1)S(1)}, u32[]{:S(2)}, u32[]{:S(2)}) async-start(bf16[32,5,128]{2,1,0:T(8,128)(2,1)} %broadcast_in_dim.61), calls=%async_computation.1 | async-start | bytes 131072 | tf_op jit(solution)/shard_map/all_to_all | solution.py:48
  48.4 0.9 copy-start.4
  52.0 22.5 %all-to-all-start.2 = ((f16[16,32,1152]{2,1,0:T(8,128)(2,1)}), f16[16,32,1152]{2,1,0:T(8,128)(2,1)S(1)}, u32[]{:S(2)}, u32[]{:S(2)}) async-start(f16[16,32,1152]{2,1,0:T(8,128)(2,1)} %bitcast.27), calls=%async_computation.2 | async-start | bytes 2359296 | tf_op jit(solution)/shard_map/all_to_all | solution.py:48
  74.5 1.1 copy-start.3
  94.5 30.2 %copy-start.2 = (f32[384,512]{1,0:T(8,128)S(1)}, f32[384,512]{1,0:T(8,128)}, u32[]{:S(2)}) copy-start(f32[384,512]{1,0:T(8,128)} %constant.15.clone) | copy-start | bytes 2359300

commit v2 on v1

--- a/solution.py
+++ b/solution.py
@@ -2,6 +2,9 @@
 import jax.numpy as jnp
 import numpy as np
 from jax import lax
+from jax.experimental import pallas as pl
+from jax.experimental.layout import Layout, with_layout_constraint
+from jax.experimental.pallas import tpu as pltpu
 from jax.sharding import Mesh
 from jax.sharding import PartitionSpec as P
 
@@ -72,6 +75,27 @@
     return jnp.where(lanes(y) == SPARE, 0.0, y) * jnp.exp2(power)
 
 
+def pick_body(cols_ref, occ_ref, vir_ref, out_ref):
+    points, no = occ_ref.shape
+    base = lax.axis_index(YZ) * points
+    column = lax.broadcasted_iota(jnp.int32, (NC, points), 0)
+    place = lax.broadcasted_iota(jnp.int32, (NC, points), 1)
+    where = jnp.full((NC, points), -1, jnp.int32)
+    for c in range(NC):
+        where = jnp.where(column == c, cols_ref[c] - base, where)
+    chosen = (where == place).astype(f32).astype(bf16)
+    occ = jnp.dot(chosen, occ_ref[...], preferred_element_type=f32)
+    vir = jnp.dot(chosen, vir_ref[...], preferred_element_type=f32)
+    rows = out_ref.shape[1]
+    for z in range(out_ref.shape[0]):
+        out_ref[z, :, :no] = occ[z * rows : (z + 1) * rows].astype(bf16)
+        out_ref[z, :, no:] = vir[z * rows : (z + 1) * rows].astype(bf16)
+
+
+def plain(x):
+    return with_layout_constraint(x, Layout(tuple(range(x.ndim))))
+
+
 def local(panel_cols, occ_orbitals, vir_orbitals, occ_energy, vir_energy, coulomb):
     moments = 0.05 * jnp.exp(0.3 * jnp.arange(NT, dtype=f32))
     points, no = occ_orbitals.shape
@@ -80,19 +104,20 @@
     times = NT * NC
     peers = lax.axis_size(ORB)
 
-    base = lax.axis_index(YZ) * points
-    positions = lax.broadcasted_iota(jnp.int32, (NC, points), 1)
-    selector = (panel_cols[:, None] - base == positions).astype(bf16)
-    pick = jnp.concatenate(
-        [jnp.dot(selector, o, preferred_element_type=f32).astype(bf16) for o in (occ_orbitals, vir_orbitals)], axis=1
-    )
-    rows = moved(pick.reshape(NC, width // 128, 128), YZ).astype(f32).sum(axis=0).astype(bf16)
-    panel = moved(jnp.broadcast_to(rows, (NC, *rows.shape)), YZ).reshape(NC, width).astype(f32)
+    zs = lax.axis_size("z")
+    pick = pl.pallas_call(
+        pick_body,
+        out_shape=jax.ShapeDtypeStruct((zs, NC // zs, width), bf16),
+        in_specs=[pl.BlockSpec(memory_space=pltpu.SMEM)] + [pl.BlockSpec(memory_space=pltpu.VMEM)] * 2,
+    )(panel_cols, occ_orbitals, vir_orbitals)
+    own = moved(pick, "z").astype(f32).sum(axis=0).astype(bf16)
+    panel = moved(jnp.broadcast_to(own, (lax.axis_size(YZ), *own.shape)), YZ)
+    panel = panel.reshape(lax.axis_size("yh"), NC, width).astype(f32).sum(axis=0)
 
     def green(orbitals, energy, panel):
         decay = jnp.exp(-energy[None, :] * moments[:, None])
         scaled = (panel[None] * decay[:, None]).astype(bf16).reshape(times, -1)
-        return lax.dot_general(orbitals, scaled, (((1,), (1,)), ((), ())), preferred_element_type=f32)
+        return plain(lax.dot_general(orbitals, scaled, (((1,), (1,)), ((), ())), preferred_element_type=f32))
 
     occ = green(occ_orbitals, occ_energy, panel[:, :no])
     vir = green(vir_orbitals, vir_energy, panel[:, no:])
@@ -119,7 +144,7 @@
     part = lax.dot_general(
         coulomb, polar, (((0,), (0,)), ((), ())), precision=lax.Precision.HIGH, preferred_element_type=f32
     )
-    blocks = moved(packed(part).reshape(NC, -1, WIDTH), YZ)
+    blocks = moved(packed(plain(part)).reshape(NC, -1, WIDTH), YZ)
     total = unpacked(blocks).sum(axis=0)
     return jnp.dot(total, RIGHT, precision=HIGHEST, preferred_element_type=f32)
 

time: 126 us -> 119 us (0.944)
  waiting for transfers between devices: 40 us -> 36.2 us
  local copies, waits for them, and re-layouts: 5.77 us -> 2.35 us
  Pallas kernels: 0 us -> 2.12 us
  starting transfers between devices: 24.7 us -> 22.7 us
    all_to_all x3, waiting for transfers between devices: 40 us -> 36.2 us  [moved(): return lax.all_to_all(x, axes, split_axis=0, concat_axis=0, tiled=True)]
    dot_general x2 -> x0, matrix products: 2.36 us -> none  [local(): jnp.dot(selector, o, preferred_element_type=f32).astype(bf16)]
    pallas_call x0 -> x1, Pallas kernels: none -> 2.12 us  [local(): pl.pallas_call(pick_body, out_shape=jax.ShapeDtypeStruct((zs, NC // zs, w...]
    all_to_all x3, starting transfers between devices: 24.7 us -> 22.7 us  [moved(): return lax.all_to_all(x, axes, split_axis=0, concat_axis=0, tiled=True)]
    convert_element_type x1, local copies, waits for them, and re-layouts: 1.76 us -> 0.02 us  [local(): panel.reshape(lax.axis_size('yh'), NC, width).astype(f32).sum(axis=0)]
    concatenate x1 -> x0, local copies, waits for them, and re-layouts: 1.67 us -> none  [local(): jnp.concatenate([(occ * jnp.exp2(-occ_power)).astype(f16), (vir * jnp.exp...]
where the time goes in v2:
time: 119 us; the launch traced here: 118 us
  blocking collectives  41.7 us (35%)
  waiting for transfers between devices  36.2 us (30%)
  starting transfers between devices  22.7 us (19%)
  matrix products  7.04 us (6%)
  other arithmetic  5.91 us (5%)
  local copies, waits for them, and re-layouts  2.35 us (2%)
  Pallas kernels  2.12 us (2%)
    all_to_all x2, blocking collectives, moved(): return lax.all_to_all(x, axes, split_axis=0, concat_axis=0, tiled=True)  41.7 us
    all_to_all x3, waiting for transfers between devices, moved(): return lax.all_to_all(x, axes, split_axis=0, concat_axis=0, tiled=True)  36.2 us
    all_to_all x3, starting transfers between devices, moved(): return lax.all_to_all(x, axes, split_axis=0, concat_axis=0, tiled=True)  22.7 us
  transfers between devices with their start and end apart: 3, of which 3 were waited for; matrix products, arithmetic and copies ran while one was open for 1% of the time, Pallas kernels for 0%

profile of v2, /device:TPU:8, one launch (start us, length us, event | category | flops | bytes accessed | tf_op | source)
XLA Modules:
  0.0 118.2 jit_solution(66719039983270100)
XLA Ops:
  0.0 0.0 copy-start
  0.0 0.0 copy-start.1
  0.0 2.1 %shard_map.82 = bf16[8,4,640]{2,1,0:T(4,128)(2,1)} custom-call(s32[32]{0:T(128)} %cols_ref.1, bf16[512,128]{1,0:T(8,128)(2,1)} %occ_ref.1, bf16[512,512]{1,0:T(8,128)(2,1)} %vir_ref.1), custom_call_target="tpu_custom_call" | custom-call | tf_op jit(solution)/shard_map/pallas_call | solution.py:108
  2.1 10.3 %all-to-all-start = ((bf16[8,4,640]{2,1,0:T(4,128)(2,1)}), bf16[8,4,640]{2,1,0:T(4,128)(2,1)S(1)}, u32[]{:S(2)}, u32[]{:S(2)}) async-start(bf16[8,4,640]{2,1,0:T(4,128)(2,1)} %shard_map.82), calls=%async_computation | async-start | bytes 81920 | tf_op jit(solution)/shard_map/all_to_all | solution.py:51
  12.4 0.7 neg.40
  13.1 0.1 multiply_exponential_fusion.1
  13.2 0.7 neg.42
  13.9 6.7 %all-to-all-done = bf16[8,4,640]{2,1,0:T(4,128)(2,1)S(1)} async-done(((bf16[8,4,640]{2,1,0:T(4,128)(2,1)}), bf16[8,4,640]{2,1,0:T(4,128)(2,1)S(1)}, u32[]{:S(2)}, u32[]{:S(2)}) %all-to-all-start) | async-done | bytes 40992 | tf_op jit(solution)/shard_map/all_to_all | solution.py:51
  20.6 0.7 broadcast_in_dim.60
  21.3 6.6 %all-to-all-start.1 = ((bf16[32,4,640]{2,1,0:T(4,128)(2,1)}), bf16[32,4,640]{2,1,0:T(4,128)(2,1)S(1)}, u32[]{:S(2)}, u32[]{:S(2)}) async-start(bf16[32,4,640]{2,1,0:T(4,128)(2,1)} %broadcast_in_dim.60), calls=%async_computation.1 | async-start | bytes 327680 | tf_op jit(solution)/shard_map/all_to_all | solution.py:51
  27.9 0.1 multiply_exponential_fusion
  28.0 12.8 %all-to-all-done.1 = bf16[32,4,640]{2,1,0:T(4,128)(2,1)S(1)} async-done(((bf16[32,4,640]{2,1,0:T(4,128)(2,1)}), bf16[32,4,640]{2,1,0:T(4,128)(2,1)S(1)}, u32[]{:S(2)}, u32[]{:S(2)}) %all-to-all-start.1) | async-done | bytes 163872 | tf_op jit(solution)/shard_map/all_to_all | solution.py:51
  40.9 0.0 copy-start.2
  40.9 0.1 multiply_convert_fusion.1
  41.0 0.0 copy-done.1
  41.0 0.6 abs_reduce_fusion
  41.6 0.2 copy-done.2
  41.8 0.4 abs_reduce_fusion.1
  42.2 0.2 multiply_convert_fusion.2
  42.3 0.2 multiply_convert_fusion
  42.5 0.2 select_convert_fusion
  42.7 1.4 %pad_maximum_fusion = f16[512,1152]{1,0:T(8,128)(2,1)} fusion(f16[512,128]{1,0:T(8,128)(2,1)S(1)} %select_convert_fusion, f16[512,512]{1,0:T(8,128)(2,1)S(1)} %multiply_convert_fusion, f16[512,512]{1,0:T(8,128)(2,1)S(1)} %multiply_convert_fusion.2), kind=kLoop, calls=%fused_computation.9 | loop fusion | flops 1179648 | bytes 2359296 | tf_op jit(solution)/shard_map/concatenate | solution.py:126
  44.1 5.8 %all-to-all-start.2 = ((f16[16,32,1152]{2,1,0:T(8,128)(2,1)}), f16[16,32,1152]{2,1,0:T(8,128)(2,1)S(1)}, u32[]{:S(2)}, u32[]{:S(2)}) async-start(f16[16,32,1152]{2,1,0:T(8,128)(2,1)} %bitcast.31), calls=%async_computation.2 | async-start | bytes 2359296 | tf_op jit(solution)/shard_map/all_to_all | solution.py:51
  49.9 16.7 %all-to-all-done.2 = f16[16,32,1152]{2,1,0:T(8,128)(2,1)S(1)} async-done(((f16[16,32,1152]{2,1,0:T(8,128)(2,1)}), f16[16,32,1152]{2,1,0:T(8,128)(2,1)S(1)}, u32[]{:S(2)}, u32[]{:S(2)}) %all-to-all-start.2) | async-done | bytes 1179680 | tf_op jit(solution)/shard_map/all_to_all | solution.py:51
  66.6 0.1 fusion.13
  66.7 0.2 copy.29
  66.9 0.2 copy.30
  67.1 0.3 multiply_reduce_fusion.1
  67.4 0.1 copy.27
  67.5 0.1 copy.26
  67.7 1.9 %abs_reduce_fusion.2 = (f32[32]{0:T(128)S(1)}, f32[32,384]{1,0:T(8,128)S(1)}) fusion(f32[512,384]{1,0:T(8,128)} %constant.28.clone, f32[32,512]{0,1:T(8,128)S(1)} %copy.26, f32[32,512]{0,1:T(8,128)S(1)} %copy.27), kind=kOutput, calls=%fused_computation.31 | convolution fusion | flops 75538400 | bytes 966784 | tf_op jit(solution)/shard_map/dot_general | solution.py:138
  69.5 0.1 fusion.10
  69.7 12.1 %all_to_all.25 = f16[16,32,384]{2,1,0:T(8,128)(2,1)S(1)} all-to-all(f16[16,32,384]{2,1,0:T(8,128)(2,1)S(1)} %broadcast_in_dim.64), channel_id=1, replica_groups=mesh['yh'=4,'z'=8,'x'=4,'yl'=2,'core'=2] {'x','yl','core'}, dimensions={0} | all-to-all | bytes 786432 | tf_op jit(solution)/shard_map/all_to_all | solution.py:51
  81.9 0.2 exponential_reduce_fusion
  82.1 0.1 select_multiply_fusion
  82.3 0.1 fusion.14
  82.4 0.1 slice_add_fusion
  82.6 0.0 copy-done
  82.6 1.9 %fusion.2 = (f32[1024]{0:T(1024)S(1)}, f32[384,1024]{0,1:T(8,128)S(1)}) fusion(f32[512,1024]{1,0:T(8,128)S(1)} %copy-done, f32[512,256]{1,0:T(8,128)S(1)} %slice.62, f32[512,128]{1,0:T(8,128)S(1)} %slice_add_fusion), kind=kOutput, calls=%fused_computation.5 | convolution fusion | flops 1208941568 | bytes 4460544 | tf_op jit(solution)/shard_map/dot_general | solution.py:144
  84.5 1.1 fusion.1
  85.6 29.5 %all_to_all.26 = f16[32,32,384]{2,1,0:T(8,128)(2,1)S(1)} all-to-all(f16[32,32,384]{2,1,0:T(8,128)(2,1)S(1)} %bitcast.32), channel_id=1, replica_groups=mesh['yh'=4,'z'=8,'x'=4,'yl'=2,'core'=2] {'yh','z'}, dimensions={0} | all-to-all | bytes 1572864 | tf_op jit(solution)/shard_map/all_to_all | solution.py:51
  115.1 0.2 slice.63
  115.3 0.3 copy.31
  115.6 0.2 multiply_reduce_fusion
  115.9 2.3 %fusion.15 = f32[32,512]{1,0:T(8,128)} fusion(f32[32,384]{1,0:T(8,128)S(1)} %multiply_reduce_fusion, f32[384,512]{1,0:T(8,128)} %constant.7.clone), kind=kOutput, calls=%fused_computation.54 | convolution fusion | flops 75497472 | bytes 901120 | tf_op jit(solution)/shard_map/dot_general | solution.py:149
  (17 shorter events, 0.3 us)
Async XLA Ops:
  0.0 82.6 %copy-start = (f32[512,1024]{1,0:T(8,128)S(1)}, f32[512,1024]{1,0:T(8,128)}, u32[]{:S(2)}) copy-start(f32[512,1024]{1,0:T(8,128)} %param.13) | copy-start | bytes 6291460
  0.0 41.0 %copy-start.1 = (bf16[512,512]{1,0:T(8,128)(2,1)S(1)}, bf16[512,512]{1,0:T(8,128)(2,1)}, u32[]{:S(2)}) copy-start(bf16[512,512]{1,0:T(8,128)(2,1)} %vir_ref.1) | copy-start | bytes 1572868
  2.1 18.4 %all-to-all-start = ((bf16[8,4,640]{2,1,0:T(4,128)(2,1)}), bf16[8,4,640]{2,1,0:T(4,128)(2,1)S(1)}, u32[]{:S(2)}, u32[]{:S(2)}) async-start(bf16[8,4,640]{2,1,0:T(4,128)(2,1)} %shard_map.82), calls=%async_computation | async-start | bytes 81920 | tf_op jit(solution)/shard_map/all_to_all | solution.py:51
  21.3 19.5 %all-to-all-start.1 = ((bf16[32,4,640]{2,1,0:T(4,128)(2,1)}), bf16[32,4,640]{2,1,0:T(4,128)(2,1)S(1)}, u32[]{:S(2)}, u32[]{:S(2)}) async-start(bf16[32,4,640]{2,1,0:T(4,128)(2,1)} %broadcast_in_dim.60), calls=%async_computation.1 | async-start | bytes 327680 | tf_op jit(solution)/shard_map/all_to_all | solution.py:51
  40.9 0.9 copy-start.2
  44.1 22.5 %all-to-all-start.2 = ((f16[16,32,1152]{2,1,0:T(8,128)(2,1)}), f16[16,32,1152]{2,1,0:T(8,128)(2,1)S(1)}, u32[]{:S(2)}, u32[]{:S(2)}) async-start(f16[16,32,1152]{2,1,0:T(8,128)(2,1)} %bitcast.31), calls=%async_computation.2 | async-start | bytes 2359296 | tf_op jit(solution)/shard_map/all_to_all | solution.py:51

commit v3 on v1

v3 whole, which is shorter than its diff:
```python
import jax
import jax.numpy as jnp
import numpy as np
from jax import lax
from jax.experimental import pallas as pl
from jax.experimental.layout import Layout, with_layout_constraint
from jax.experimental.pallas import tpu as pltpu
from jax.sharding import Mesh
from jax.sharding import PartitionSpec as P

NT = 16
NF = 16
NC = 32
RANK = 10
TWICE = 2
WIDTH = 384
SPARE = 127
SLOTS = 8
YZ = ("yh", "z")
ORB = ("x", "yl", "core")
HIGH = lax.Precision.HIGH
f32, f16, bf16 = jnp.float32, jnp.float16, jnp.bfloat16


def factors():
    moments = 0.05 * np.exp(0.3 * np.arange(NT))
    freqs = 0.1 * np.exp(0.3 * np.arange(NF))
    table = 0.3 * moments[None, :] * np.cos(freqs[:, None] * moments[None, :])
    u = np.linalg.svd(table)[0][:, :RANK]
    rates = np.exp(np.linspace(np.log(0.1), np.log(5.0), 400))
    typical = u.T @ table @ np.exp(-moments[:, None] * rates[None, :])
    turn = np.linalg.eigh(typical @ typical.T)[1][:, ::-1]
    up = u @ turn
    down = up.T @ table
    slots = [*range(TWICE), *range(TWICE), *range(TWICE, RANK)]
    left = np.zeros((NT, NC, len(slots), NC))
    right = np.zeros((len(slots), NC, NC, NF))
    for k, j in enumerate(slots):
        for c in range(NC):
            left[:, c, k, c] = down[j]
            right[k, c, c, :] = up[:, j]
    return (
        left.reshape(NT * NC, WIDTH).astype(np.float32),
        right.reshape(WIDTH, NC * NF).astype(np.float32),
    )


LEFT, RIGHT = factors()


def moved(x, axes):
    return lax.all_to_all(x, axes, split_axis=0, concat_axis=0, tiled=True)


def power_of(x):
    top = jnp.max(jnp.abs(x), axis=-1, keepdims=True)
    return jnp.ceil(jnp.log2(jnp.maximum(top, 1e-30))) - 14.0


def lanes(x):
    return lax.broadcasted_iota(jnp.int32, x.shape, x.ndim - 1)


def at_lane(x, lane):
    return jnp.where(lanes(x) == lane, x, 0).astype(f32).sum(axis=-1, keepdims=True)


def packed(x):
    power = power_of(x)
    scaled = x * jnp.exp2(-power)
    lane = lanes(x)
    rest = scaled - lax.reduce_precision(scaled, 5, 10)
    low = (lane >= 64) & (lane < 128)
    return jnp.where(lane == SPARE, power, jnp.where(low, rest, scaled)).astype(f16)


def unpacked(y):
    power = at_lane(y[..., :128], SPARE)
    y = y.astype(f32)
    return jnp.where(lanes(y) == SPARE, 0.0, y) * jnp.exp2(power)


def pick_body(cols_ref, occ_ref, vir_ref, out_ref):
    points, no = occ_ref.shape
    base = lax.axis_index(YZ) * points
    slot = lax.broadcasted_iota(jnp.int32, (SLOTS, points), 0)
    place = lax.broadcasted_iota(jnp.int32, (SLOTS, points), 1)
    where = jnp.full((SLOTS, points), -1, jnp.int32)
    found = jnp.int32(0)
    for c in range(NC):
        row = cols_ref[c] - base
        here = (row >= 0) & (row < points)
        where = jnp.where(slot == jnp.where(here, found, -1), row, where)
        found = found + here.astype(jnp.int32)
    chosen = (where == place).astype(f32).astype(bf16)
    occ = jnp.dot(chosen, occ_ref[...], preferred_element_type=f32).astype(bf16)
    vir = jnp.dot(chosen, vir_ref[...], preferred_element_type=f32).astype(bf16)
    for k in range(out_ref.shape[0]):
        out_ref[k, :, :no] = occ
        out_ref[k, :, no:] = vir


def plain(x):
    return with_layout_constraint(x, Layout(tuple(range(x.ndim))))


def panel_rows(panel_cols, occ_orbitals, vir_orbitals):
    points, no = occ_orbitals.shape
    width = no + vir_orbitals.shape[1]
    blocks = lax.axis_size(YZ)
    sent = pl.pallas_call(
        pick_body,
        out_shape=jax.ShapeDtypeStruct((blocks, SLOTS, width), bf16),
        in_specs=[pl.BlockSpec(memory_space=pltpu.SMEM)] + [pl.BlockSpec(memory_space=pltpu.VMEM)] * 2,
    )(panel_cols, occ_orbitals, vir_orbitals)
    got = moved(sent, YZ).reshape(blocks * SLOTS, width)
    block = panel_cols // points
    earlier = np.tril(np.ones((NC, NC), bool), -1)
    slot = ((block[:, None] == block[None, :]) & earlier).astype(jnp.int32).sum(axis=1)
    source = lax.broadcasted_iota(jnp.int32, (NC, blocks * SLOTS), 1)
    chosen = ((block * SLOTS + slot)[:, None] == source).astype(bf16)
    few = jnp.dot(chosen, got, preferred_element_type=f32)

    def summed():
        zs = lax.axis_size("z")
        positions = lax.broadcasted_iota(jnp.int32, (NC, points), 1)
        selector = (panel_cols[:, None] - lax.axis_index(YZ) * points == positions).astype(bf16)
        pick = [jnp.dot(selector, o, preferred_element_type=f32).astype(bf16) for o in (occ_orbitals, vir_orbitals)]
        pick = jnp.concatenate(pick, axis=1).reshape(zs, NC // zs, width)
        own = moved(pick, "z").astype(f32).sum(axis=0).astype(bf16)
        rows = moved(jnp.broadcast_to(own, (blocks, *own.shape)), YZ)
        return rows.reshape(-1, NC, width).astype(f32).sum(axis=0)

    return lax.cond(jnp.any(slot >= SLOTS), summed, lambda: few)


def local(panel_cols, occ_orbitals, vir_orbitals, occ_energy, vir_energy, coulomb):
    moments = 0.05 * jnp.exp(0.3 * jnp.arange(NT, dtype=f32))
    points, no = occ_orbitals.shape
    times = NT * NC
    peers = lax.axis_size(ORB)
    panel = panel_rows(panel_cols, occ_orbitals, vir_orbitals)

    def green(orbitals, energy, panel, first):
        decay = jnp.exp(-energy[None, :] * moments[:, None])
        decay = jnp.pad(decay, ((first, 2 * NT + 4 - NT - first), (0, 0)))
        scaled = (panel[None] * decay[:, None]).astype(bf16).reshape(2 * times + 128, -1)
        return lax.dot_general(orbitals, scaled, (((1,), (1,)), ((), ())), preferred_element_type=f32)

    both = green(occ_orbitals, occ_energy, panel[:, :no], 0) + green(vir_orbitals, vir_energy, panel[:, no:], NT)
    both = plain(both)
    power = power_of(both)
    sent = jnp.where(lanes(both) == 2 * times, power, both * jnp.exp2(-power)).astype(f16)
    got = moved(sent.reshape(peers, points // peers, -1), ORB)
    power = at_lane(got[..., 2 * times :], 0)
    both = (got.astype(f32) * jnp.exp2(power)).sum(axis=0)
    product = both[:, :times] * both[:, times : 2 * times]
    polar = packed(jnp.dot(product, LEFT, precision=HIGH, preferred_element_type=f32))
    polar = moved(jnp.broadcast_to(polar, (peers, *polar.shape)), ORB)
    polar = unpacked(polar.reshape(points, WIDTH))
    pair = polar[:, :128]
    pair = pair + jnp.roll(pair, 64, axis=1)
    polar = jnp.concatenate([pair, polar[:, 128:]], axis=1)
    part = lax.dot_general(coulomb, polar, (((0,), (0,)), ((), ())), precision=HIGH, preferred_element_type=f32)
    blocks = moved(packed(plain(part)).reshape(NC, -1, WIDTH), YZ)
    total = unpacked(blocks).sum(axis=0)
    return jnp.dot(total, RIGHT, precision=HIGH, preferred_element_type=f32)


def solution(mesh):
    finer = Mesh(mesh.devices.reshape(4, 8, 4, 2, 2), (*YZ, *ORB))
    placed = (P(), P(YZ, ORB), P(YZ, ORB), P(ORB), P(ORB), P(YZ, ORB))
    return jax.shard_map(local, mesh=finer, in_specs=placed, out_specs=P(ORB + YZ, None), check_vma=False)
```

time: 126 us -> 111 us (0.88)
  blocking collectives: 41.7 us -> 31.3 us
  local copies, waits for them, and re-layouts: 5.77 us -> 1.65 us
  Pallas kernels: 0 us -> 2.29 us
  waiting for transfers between devices: 40 us -> 38 us
  other arithmetic: 7.03 us -> 5.37 us
  matrix products: 6.5 us -> 4.96 us
  starting transfers between devices: 24.7 us -> 26.2 us
    all_to_all x2 -> x1, blocking collectives: 41.7 us -> 31.3 us  [moved(): return lax.all_to_all(x, axes, split_axis=0, concat_axis=0, tiled=True)]
    pallas_call x0 -> x1, Pallas kernels: none -> 2.29 us  [panel_rows(): pl.pallas_call(pick_body, out_shape=jax.ShapeDtypeStruct((blocks, SLOTS,...]
    dot_general x5 -> x4, matrix products: 5.71 us -> 3.51 us  [the longest x1 1.93 us: local(): lax.dot_general(coulomb, polar, (((0,), (0,)), ((), ())), precision=HIGH,...]
    all_to_all x3, waiting for transfers between devices: 40 us -> 38 us  [moved(): return lax.all_to_all(x, axes, split_axis=0, concat_axis=0, tiled=True)]
    convert_element_type x1 -> x0, local copies, waits for them, and re-layouts: 1.76 us -> none  [packed(): jnp.where(lane == SPARE, power, jnp.where(low, rest, scaled)).astype(f16)]
    concatenate x1 -> x0, local copies, waits for them, and re-layouts: 1.67 us -> none  [local(): jnp.concatenate([(occ * jnp.exp2(-occ_power)).astype(f16), (vir * jnp.exp...]
    all_to_all x3, starting transfers between devices: 24.7 us -> 26.2 us  [moved(): return lax.all_to_all(x, axes, split_axis=0, concat_axis=0, tiled=True)]
    neg x2, other arithmetic: 1.34 us -> 0.01 us  [green(): decay = jnp.exp(-energy[None, :] * moments[:, None])]
where the time goes in v3:
time: 111 us
  waiting for transfers between devices  38 us (34%)
  blocking collectives  31.3 us (28%)
  starting transfers between devices  26.2 us (24%)
  other arithmetic  5.37 us (5%)
  matrix products  4.96 us (4%)
  Pallas kernels  2.29 us (2%)
  local copies, waits for them, and re-layouts  1.65 us (1%)
    all_to_all x3, waiting for transfers between devices, moved(): return lax.all_to_all(x, axes, split_axis=0, concat_axis=0, tiled=True)  38 us
    all_to_all x1, blocking collectives, moved(): return lax.all_to_all(x, axes, split_axis=0, concat_axis=0, tiled=True)  31.3 us
    all_to_all x3, starting transfers between devices, moved(): return lax.all_to_all(x, axes, split_axis=0, concat_axis=0, tiled=True)  26.2 us
    pallas_call x1, Pallas kernels, panel_rows(): pl.pallas_call(pick_body, out_shape=jax.ShapeDtypeStruct((blocks, SLOTS,...  2.29 us
  transfers between devices with their start and end apart: 3, of which 3 were waited for; matrix products, arithmetic and copies ran while one was open for 1% of the time, Pallas kernels for 0%

profile of v3, /device:TPU:8, one launch (start us, length us, event | category | flops | bytes accessed | tf_op | source)
XLA Modules:
  0.0 110.7 jit_solution(14937323013514725511)
XLA Ops:
  0.0 0.0 copy-start
  0.0 0.0 copy-start.5
  0.0 0.0 copy-start.7
  0.0 0.0 copy-start.4
  0.0 0.0 copy-start.1
  0.0 0.0 copy-start.6
  0.0 0.0 copy-start.8
  0.1 2.3 %shard_map.91 = bf16[32,8,640]{2,1,0:T(8,128)(2,1)} custom-call(s32[32]{0:T(128)} %cols_ref.1, bf16[512,128]{1,0:T(8,128)(2,1)} %occ_ref.1, bf16[512,512]{1,0:T(8,128)(2,1)} %vir_ref.1), custom_call_target="tpu_custom_call" | custom-call | tf_op jit(solution)/shard_map/pallas_call | solution.py:111
  2.3 15.1 %all-to-all-start.2 = ((bf16[32,8,640]{2,1,0:T(8,128)(2,1)}), bf16[32,8,640]{2,1,0:T(8,128)(2,1)S(1)}, u32[]{:S(2)}, u32[]{:S(2)}) async-start(bf16[32,8,640]{2,1,0:T(8,128)(2,1)} %shard_map.91), calls=%async_computation.2 | async-start | bytes 655360 | tf_op jit(solution)/shard_map/all_to_all | solution.py:52
  17.4 0.0 copy-done.7
  17.5 0.0 copy-done.6
  17.5 0.0 copy-done.5
  17.5 0.2 convert_reduce_fusion.3
  17.7 0.1 multiply_exponential_fusion
  17.8 0.6 compare_reduce_fusion
  19.0 0.0 copy-done.8
  19.1 0.1 multiply_exponential_fusion.3
  19.2 13.0 %all-to-all-done.2 = bf16[32,8,640]{2,1,0:T(8,128)(2,1)S(1)} async-done(((bf16[32,8,640]{2,1,0:T(8,128)(2,1)}), bf16[32,8,640]{2,1,0:T(8,128)(2,1)S(1)}, u32[]{:S(2)}, u32[]{:S(2)}) %all-to-all-start.2) | async-done | bytes 327712 | tf_op jit(solution)/shard_map/all_to_all | solution.py:52
  32.1 0.0 copy-done.4
  32.1 0.0 copy-done.1
  32.1 0.2 fusion.10
  32.4 0.3 multiply_convert_fusion
  32.7 0.9 fusion.19
  33.6 0.1 multiply_convert_fusion.1
  33.6 0.6 abs_reduce_fusion
  34.2 1.4 %select_convert_fusion = f16[512,1152]{1,0:T(8,128)(2,1)} fusion(f32[512,1152]{1,0:T(8,128)S(1)} %get-tuple-element.27, f32[512]{0:T(512)S(1)} %get-tuple-element.25, f32[512]{0:T(512)S(1)} %get-tuple-element.24, pred[1152]{0:T(1024)(128)(4,1)S(1)} %iota_compare_fusion.5), kind=kLoop, calls=%fused_computation.11 | loop fusion | flops 1769472 | bytes 3544192 | tf_op jit(solution)/shard_map/convert_element_type | solution.py:153
  35.6 6.5 %all-to-all-start.3 = ((f16[16,32,1152]{2,1,0:T(8,128)(2,1)}), f16[16,32,1152]{2,1,0:T(8,128)(2,1)S(1)}, u32[]{:S(2)}, u32[]{:S(2)}) async-start(f16[16,32,1152]{2,1,0:T(8,128)(2,1)} %bitcast.29), calls=%async_computation.3 | async-start | bytes 2359296 | tf_op jit(solution)/shard_map/all_to_all | solution.py:52
  42.1 16.7 %all-to-all-done.3 = f16[16,32,1152]{2,1,0:T(8,128)(2,1)S(1)} async-done(((f16[16,32,1152]{2,1,0:T(8,128)(2,1)}), f16[16,32,1152]{2,1,0:T(8,128)(2,1)S(1)}, u32[]{:S(2)}, u32[]{:S(2)}) %all-to-all-start.3) | async-done | bytes 1179680 | tf_op jit(solution)/shard_map/all_to_all | solution.py:52
  58.8 0.0 copy-start.3
  58.8 0.1 convert_reduce_fusion.2
  59.0 0.3 multiply_reduce_fusion
  59.3 0.7 copy-done.3
  59.9 0.4 abs_reduce_fusion.1
  60.4 0.1 fusion.14
  60.5 0.8 broadcast_in_dim.73
  61.3 4.7 %all-to-all-start.4 = ((f16[16,32,384]{2,1,0:T(8,128)(2,1)}), f16[16,32,384]{2,1,0:T(8,128)(2,1)S(1)}, u32[]{:S(2)}, u32[]{:S(2)}) async-start(f16[16,32,384]{2,1,0:T(8,128)(2,1)} %broadcast_in_dim.73), calls=%async_computation.4 | async-start | bytes 786432 | tf_op jit(solution)/shard_map/all_to_all | solution.py:52
  66.0 8.3 %all-to-all-done.4 = f16[16,32,384]{2,1,0:T(8,128)(2,1)S(1)} async-done(((f16[16,32,384]{2,1,0:T(8,128)(2,1)}), f16[16,32,384]{2,1,0:T(8,128)(2,1)S(1)}, u32[]{:S(2)}, u32[]{:S(2)}) %all-to-all-start.4) | async-done | bytes 393248 | tf_op jit(solution)/shard_map/all_to_all | solution.py:52
  74.3 0.1 convert_reduce_fusion.1
  74.5 0.1 select_multiply_fusion
  74.6 0.1 fusion.18
  74.8 0.1 slice_add_fusion
  75.0 0.0 copy-done
  75.0 1.9 %fusion.5 = (f32[1024]{0:T(1024)S(1)}, f32[384,1024]{0,1:T(8,128)S(1)}) fusion(f32[512,1024]{1,0:T(8,128)S(1)} %copy-done, f32[512,256]{1,0:T(8,128)S(1)} %slice.57, f32[512,128]{1,0:T(8,128)S(1)} %slice_add_fusion), kind=kOutput, calls=%fused_computation.18 | convolution fusion | flops 1208941568 | bytes 4460544 | tf_op jit(solution)/shard_map/dot_general | solution.py:164
  76.9 1.1 fusion.4
  78.0 0.0 copy-start.2
  78.0 31.3 %all_to_all.30 = f16[32,32,384]{2,1,0:T(8,128)(2,1)S(1)} all-to-all(f16[32,32,384]{2,1,0:T(8,128)(2,1)S(1)} %bitcast.30), channel_id=1, replica_groups=mesh['yh'=4,'z'=8,'x'=4,'yl'=2,'core'=2] {'yh','z'}, dimensions={0} | all-to-all | bytes 1572864 | tf_op jit(solution)/shard_map/all_to_all | solution.py:52
  109.3 0.2 convert_reduce_fusion
  109.5 0.2 multiply_reduce_fusion.1
  109.8 0.0 copy-done.2
  109.8 0.9 fusion.20
  (21 shorter events, 0.2 us)
Async XLA Ops:
  0.0 75.0 %copy-start = (f32[512,1024]{1,0:T(8,128)S(1)}, f32[512,1024]{1,0:T(8,128)}, u32[]{:S(2)}) copy-start(f32[512,1024]{1,0:T(8,128)} %param.16) | copy-start | bytes 6291460
  0.0 17.5 %copy-start.5 = (pred[32,32]{1,0:T(32,128)(4,1)S(1)}, pred[32,32]{1,0:T(32,128)(4,1)}, u32[]{:S(2)}) copy-start(pred[32,32]{1,0:T(32,128)(4,1)} %constant.94.clone) | copy-start | bytes 3076
  0.0 17.4 %copy-start.7 = (s32[32]{0:T(128)S(1)}, s32[32]{0:T(128)}, u32[]{:S(2)}) copy-start(s32[32]{0:T(128)} %cols_ref.1) | copy-start | bytes 388
  0.0 32.1 %copy-start.4 = (bf16[512,128]{1,0:T(8,128)(2,1)S(1)}, bf16[512,128]{1,0:T(8,128)(2,1)}, u32[]{:S(2)}) copy-start(bf16[512,128]{1,0:T(8,128)(2,1)} %occ_ref.1) | copy-start | bytes 393220
  0.0 32.1 %copy-start.1 = (bf16[512,512]{1,0:T(8,128)(2,1)S(1)}, bf16[512,512]{1,0:T(8,128)(2,1)}, u32[]{:S(2)}) copy-start(bf16[512,512]{1,0:T(8,128)(2,1)} %vir_ref.1) | copy-start | bytes 1572868
  0.0 17.4 %copy-start.6 = (f32[512]{0:T(512)S(1)}, f32[512]{0:T(512)}, u32[]{:S(2)}) copy-start(f32[512]{0:T(512)} %param.15) | copy-start | bytes 6148
  0.0 19.0 %copy-start.8 = (f32[128]{0:T(128)S(1)}, f32[128]{0:T(128)}, u32[]{:S(2)}) copy-start(f32[128]{0:T(128)} %param.14) | copy-start | bytes 1540
  2.3 29.8 %all-to-all-start.2 = ((bf16[32,8,640]{2,1,0:T(8,128)(2,1)}), bf16[32,8,640]{2,1,0:T(8,128)(2,1)S(1)}, u32[]{:S(2)}, u32[]{:S(2)}) async-start(bf16[32,8,640]{2,1,0:T(8,128)(2,1)} %shard_map.91), calls=%async_computation.2 | async-start | bytes 655360 | tf_op jit(solution)/shard_map/all_to_all | solution.py:52
  35.6 23.2 %all-to-all-start.3 = ((f16[16,32,1152]{2,1,0:T(8,128)(2,1)}), f16[16,32,1152]{2,1,0:T(8,128)(2,1)S(1)}, u32[]{:S(2)}, u32[]{:S(2)}) async-start(f16[16,32,1152]{2,1,0:T(8,128)(2,1)} %bitcast.29), calls=%async_computation.3 | async-start | bytes 2359296 | tf_op jit(solution)/shard_map/all_to_all | solution.py:52
  58.8 1.1 %copy-start.3 = (f32[512,384]{1,0:T(8,128)S(1)}, f32[512,384]{1,0:T(8,128)}, u32[]{:S(2)}) copy-start(f32[512,384]{1,0:T(8,128)} %constant.95.clone) | copy-start | bytes 2359300
  61.3 13.0 %all-to-all-start.4 = ((f16[16,32,384]{2,1,0:T(8,128)(2,1)}), f16[16,32,384]{2,1,0:T(8,128)(2,1)S(1)}, u32[]{:S(2)}, u32[]{:S(2)}) async-start(f16[16,32,384]{2,1,0:T(8,128)(2,1)} %broadcast_in_dim.73), calls=%async_computation.4 | async-start | bytes 786432 | tf_op jit(solution)/shard_map/all_to_all | solution.py:52
  78.0 31.8 %copy-start.2 = (f32[384,512]{1,0:T(8,128)S(1)}, f32[384,512]{1,0:T(8,128)}, u32[]{:S(2)}) copy-start(f32[384,512]{1,0:T(8,128)} %constant.96.clone) | copy-start | bytes 2359300

commit v4 on v3

--- a/solution.py
+++ b/solution.py
@@ -61,10 +61,6 @@
     return lax.broadcasted_iota(jnp.int32, x.shape, x.ndim - 1)
 
 
-def at_lane(x, lane):
-    return jnp.where(lanes(x) == lane, x, 0).astype(f32).sum(axis=-1, keepdims=True)
-
-
 def packed(x):
     power = power_of(x)
     scaled = x * jnp.exp2(-power)
@@ -75,7 +71,7 @@
 
 
 def unpacked(y):
-    power = at_lane(y[..., :128], SPARE)
+    power = y[..., SPARE : SPARE + 1].astype(f32)
     y = y.astype(f32)
     return jnp.where(lanes(y) == SPARE, 0.0, y) * jnp.exp2(power)
 
@@ -131,15 +127,39 @@
         rows = moved(jnp.broadcast_to(own, (blocks, *own.shape)), YZ)
         return rows.reshape(-1, NC, width).astype(f32).sum(axis=0)
 
-    return lax.cond(jnp.any(slot >= SLOTS), summed, lambda: few)
+    return lax.cond(jnp.any(slot >= SLOTS), summed, lambda: few), sent
+
+
+def in_three(e):
+    hi = lax.reduce_precision(e, 8, 7)
+    mid = lax.reduce_precision(e - hi, 8, 7)
+    return jnp.stack([hi, mid, e - hi - mid]).astype(bf16)
+
+
+def to_other_core(x):
+    return lax.ppermute(x, "core", [(0, 1), (1, 0)])
 
 
 def local(panel_cols, occ_orbitals, vir_orbitals, occ_energy, vir_energy, coulomb):
     moments = 0.05 * jnp.exp(0.3 * jnp.arange(NT, dtype=f32))
     points, no = occ_orbitals.shape
+    half = points // 2
     times = NT * NC
-    peers = lax.axis_size(ORB)
-    panel = panel_rows(panel_cols, occ_orbitals, vir_orbitals)
+    core = lax.axis_index("core")
+
+    def rows_of(x, k):
+        return jnp.where(k == 0, x[:half], x[half:])
+
+    panel, picked = panel_rows(panel_cols, occ_orbitals, vir_orbitals)
+    occ_late, vir_late, _ = lax.optimization_barrier((occ_orbitals, vir_orbitals, picked))
+    energies = in_three(jnp.concatenate([occ_energy, vir_energy]))
+    theirs = jnp.concatenate([rows_of(occ_late, 1 - core), rows_of(vir_late, 1 - core)], axis=1)
+    theirs = jnp.concatenate([theirs, jnp.pad(energies, ((0, 5), (0, 0)))], axis=0)
+    theirs = to_other_core(theirs)
+    other_panel = to_other_core(panel.astype(bf16)).astype(f32)
+    pieces = theirs[half : half + 3].astype(f32)
+    other_energy = pieces[0] + pieces[1] + pieces[2]
+    theirs = theirs[:half]
 
     def green(orbitals, energy, panel, first):
         decay = jnp.exp(-energy[None, :] * moments[:, None])
@@ -147,16 +167,20 @@
         scaled = (panel[None] * decay[:, None]).astype(bf16).reshape(2 * times + 128, -1)
         return lax.dot_general(orbitals, scaled, (((1,), (1,)), ((), ())), preferred_element_type=f32)
 
-    both = green(occ_orbitals, occ_energy, panel[:, :no], 0) + green(vir_orbitals, vir_energy, panel[:, no:], NT)
+    both = green(rows_of(vir_orbitals, core), vir_energy, panel[:, no:], NT)
+    both += green(rows_of(occ_orbitals, core), occ_energy, panel[:, :no], 0)
+    both += green(theirs[:, no:], other_energy[no:], other_panel[:, no:], NT)
+    both += green(theirs[:, :no], other_energy[:no], other_panel[:, :no], 0)
     both = plain(both)
     power = power_of(both)
     sent = jnp.where(lanes(both) == 2 * times, power, both * jnp.exp2(-power)).astype(f16)
-    got = moved(sent.reshape(peers, points // peers, -1), ORB)
-    power = at_lane(got[..., 2 * times :], 0)
+    peers = lax.axis_size(("x", "yl"))
+    got = moved(sent.reshape(peers, half // peers, -1), ("x", "yl"))
+    power = got[..., 2 * times : 2 * times + 1].astype(f32)
     both = (got.astype(f32) * jnp.exp2(power)).sum(axis=0)
     product = both[:, :times] * both[:, times : 2 * times]
     polar = packed(jnp.dot(product, LEFT, precision=HIGH, preferred_element_type=f32))
-    polar = moved(jnp.broadcast_to(polar, (peers, *polar.shape)), ORB)
+    polar = moved(jnp.broadcast_to(polar, (lax.axis_size(ORB), *polar.shape)), ("core", "x", "yl"))
     polar = unpacked(polar.reshape(points, WIDTH))
     pair = polar[:, :128]
     pair = pair + jnp.roll(pair, 64, axis=1)

time: 111 us -> 108 us (0.973)
  waiting for transfers between devices: 38 us -> 20.3 us
  blocking collectives: 31.3 us -> 42.8 us
  matrix products: 4.96 us -> 7.18 us
    all_to_all x3 -> x2, waiting for transfers between devices: 38 us -> 20.2 us  [moved(): return lax.all_to_all(x, axes, split_axis=0, concat_axis=0, tiled=True)]
    all_to_all x1 -> x2, blocking collectives: 31.3 us -> 42.8 us  [moved(): return lax.all_to_all(x, axes, split_axis=0, concat_axis=0, tiled=True)]
    all_to_all x3 -> x2, starting transfers between devices: 26.2 us -> 21.6 us  [moved(): return lax.all_to_all(x, axes, split_axis=0, concat_axis=0, tiled=True)]
    ppermute x0 -> x2, starting transfers between devices: none -> 3.84 us  [to_other_core(): return lax.ppermute(x, 'core', [(0, 1), (1, 0)])]
    dot_general x2 -> x4, matrix products: 1.45 us -> 3.6 us  [green(): lax.dot_general(orbitals, scaled, (((1,), (1,)), ((), ())), preferred_ele...]
  transfers between devices with their start and end apart: 3 -> 4, of which waited for: 3 -> 3; matrix products, arithmetic and copies ran while one was open for 1% -> 3% of each run, Pallas kernels for 0% -> 0%
where the time goes in v4:
time: 108 us; the launch traced here: 107 us
  blocking collectives  42.8 us (40%)
  starting transfers between devices  25.5 us (24%)
  waiting for transfers between devices  20.3 us (19%)
  matrix products  7.18 us (7%)
  other arithmetic  5.93 us (5%)
  Pallas kernels  2.33 us (2%)
  local copies, waits for them, and re-layouts  2.03 us (2%)
  between operations  1.1 us (1%)
    all_to_all x2, blocking collectives, moved(): return lax.all_to_all(x, axes, split_axis=0, concat_axis=0, tiled=True)  42.8 us
    all_to_all x2, starting transfers between devices, moved(): return lax.all_to_all(x, axes, split_axis=0, concat_axis=0, tiled=True)  21.6 us
    all_to_all x2, waiting for transfers between devices, moved(): return lax.all_to_all(x, axes, split_axis=0, concat_axis=0, tiled=True)  20.2 us
    ppermute x2, starting transfers between devices, to_other_core(): return lax.ppermute(x, 'core', [(0, 1), (1, 0)])  3.84 us
    dot_general x4, matrix products, green(): lax.dot_general(orbitals, scaled, (((1,), (1,)), ((), ())), preferred_ele...  3.6 us
    pallas_call x1, Pallas kernels, panel_rows(): pl.pallas_call(pick_body, out_shape=jax.ShapeDtypeStruct((blocks, SLOTS,...  2.33 us
  transfers between devices with their start and end apart: 4, of which 3 were waited for; matrix products, arithmetic and copies ran while one was open for 3% of the time, Pallas kernels for 0%

profile of v4, /device:TPU:8, one launch (start us, length us, event | category | flops | bytes accessed | tf_op | source)
XLA Modules:
  0.0 107.2 jit_solution(13340013298131056116)
XLA Ops:
  0.0 0.0 copy-start
  0.0 0.0 copy-start.2
  0.0 0.0 copy-start.1
  0.0 0.0 copy-start.8
  0.0 0.0 copy-start.5
  0.0 2.3 %shard_map.91 = bf16[32,8,640]{2,1,0:T(8,128)(2,1)} custom-call(s32[32]{0:T(128)} %cols_ref.1, bf16[512,128]{1,0:T(8,128)(2,1)} %occ_ref.1, bf16[512,512]{1,0:T(8,128)(2,1)} %vir_ref.1), custom_call_target="tpu_custom_call" | custom-call | tf_op jit(solution)/shard_map/pallas_call | solution.py:107
  2.4 0.0 copy-start.7
  2.4 0.0 copy-start.6
  2.4 15.2 %all-to-all-start.2 = ((bf16[32,8,640]{2,1,0:T(8,128)(2,1)}), bf16[32,8,640]{2,1,0:T(8,128)(2,1)S(1)}, u32[]{:S(2)}, u32[]{:S(2)}) async-start(bf16[32,8,640]{2,1,0:T(8,128)(2,1)} %shard_map.91), calls=%async_computation.2 | async-start | bytes 655360 | tf_op jit(solution)/shard_map/all_to_all | solution.py:52
  17.6 0.0 copy-done.1
  17.6 0.0 copy-done.2
  17.7 0.0 copy-done.8
  17.7 0.0 copy-done.5
  17.8 1.9 %collective-permute-start = (bf16[264,640]{1,0:T(8,128)(2,1)S(1)}, bf16[264,640]{1,0:T(8,128)(2,1)}, u32[]{:S(2)}, u32[]{:S(2)}) collective-permute-start(bf16[264,640]{1,0:T(8,128)(2,1)S(1)} %pad_maximum_fusion.1), channel_id=1, source_target_pairs={{0,1},{1,0},{2,3},{3,2},{4,5},{5,4},{6,7},{7,6},{8,9},{9,8},{10,11... | collective-permute-start | bytes 1013768 | tf_op jit(solution)/shard_map/ppermute | solution.py:140
  19.7 0.0 copy-done.7
  19.7 0.0 copy-done.6
  19.7 0.2 convert_reduce_fusion
  19.9 0.6 compare_reduce_fusion
  21.3 0.2 collective-permute-done
  21.4 0.7 slice_convert_fusion
  22.2 0.1 multiply_exponential_fusion
  22.3 0.1 multiply_exponential_fusion.3
  22.4 9.9 %all-to-all-done.2 = bf16[32,8,640]{2,1,0:T(8,128)(2,1)S(1)} async-done(((bf16[32,8,640]{2,1,0:T(8,128)(2,1)}), bf16[32,8,640]{2,1,0:T(8,128)(2,1)S(1)}, u32[]{:S(2)}, u32[]{:S(2)}) %all-to-all-start.2) | async-done | bytes 327712 | tf_op jit(solution)/shard_map/all_to_all | solution.py:52
  32.3 0.2 fusion.10
  32.6 1.9 %collective-permute-start.1 = (bf16[32,640]{1,0:T(8,128)(2,1)S(1)}, bf16[32,640]{1,0:T(8,128)(2,1)S(1)}, u32[]{:S(2)}, u32[]{:S(2)}) collective-permute-start(bf16[32,640]{1,0:T(8,128)(2,1)S(1)} %convert_element_type.101), channel_id=1, source_target_pairs={{0,1},{1,0},{2,3},{3,2},{4,5},{5,4},{6,7},{7,6},{8,9},{9,8},{10,11... | collective-permute-start | bytes 122888 | tf_op jit(solution)/shard_map/ppermute | solution.py:140
  34.5 0.3 multiply_convert_fusion.1
  34.8 0.5 fusion.15
  35.4 0.1 multiply_convert_fusion.3
  35.4 0.3 convolution_add_fusion
  35.7 0.0 collective-permute-done.1
  35.8 0.1 multiply_convert_fusion.2
  35.8 0.3 multiply_convert_fusion
  36.2 1.2 %fusion.20 = f32[256,1152]{1,0:T(8,128)S(1)} fusion(bf16[1152,128]{1,0:T(8,128)(2,1)S(1)} %bitcast.42, bf16[264,640]{1,0:T(8,128)(2,1)} %collective-permute-done), kind=kOutput, calls=%fused_computation.44 | convolution fusion | flops 75497472 | bytes 1540096 | tf_op jit(solution)/shard_map/dot_general | solution.py:168
  37.3 1.6 %abs_reduce_fusion = (f32[256]{0:T(256)S(1)}, f32[256,1152]{1,0:T(8,128)S(1)}) fusion(f32[256,1152]{1,0:T(8,128)S(1)} %fusion.20, f32[256,1152]{1,0:T(8,128)S(1)} %convolution_add_fusion, bf16[1152,512]{1,0:T(8,128)(2,1)S(1)} %bitcast.38, bf16[264,640]{1,0:T(8,128)(2,1)} %collective-permute-done), kind=kOutput, calls=%fused_computation.21 | convolution fusion | flops 303169280 | bytes 4981760 | tf_op jit(solution)/shard_map/dot_general | solution.py:168
  38.9 1.0 select_convert_fusion
  40.0 6.4 %all-to-all-start.3 = ((f16[8,32,1152]{2,1,0:T(8,128)(2,1)}), f16[8,32,1152]{2,1,0:T(8,128)(2,1)S(1)}, u32[]{:S(2)}, u32[]{:S(2)}) async-start(f16[8,32,1152]{2,1,0:T(8,128)(2,1)} %bitcast.9), calls=%async_computation.3 | async-start | bytes 1179648 | tf_op jit(solution)/shard_map/all_to_all | solution.py:52
  46.4 0.0 copy-start.4
  46.4 10.3 %all-to-all-done.3 = f16[8,32,1152]{2,1,0:T(8,128)(2,1)S(1)} async-done(((f16[8,32,1152]{2,1,0:T(8,128)(2,1)}), f16[8,32,1152]{2,1,0:T(8,128)(2,1)S(1)}, u32[]{:S(2)}, u32[]{:S(2)}) %all-to-all-start.3) | async-done | bytes 589856 | tf_op jit(solution)/shard_map/all_to_all | solution.py:52
  56.7 0.1 copy.25
  56.8 0.2 multiply_reduce_fusion.1
  57.1 0.1 copy.26
  57.2 0.1 copy.27
  57.4 0.0 copy-done.4
  57.4 0.5 abs_reduce_fusion.1
  57.9 0.1 fusion.27
  58.1 11.8 %all_to_all.30 = f16[16,32,384]{2,1,0:T(8,128)(2,1)S(1)} all-to-all(f16[16,32,384]{2,1,0:T(8,128)(2,1)S(1)} %broadcast_in_dim.37), channel_id=1, replica_groups=mesh['yh'=4,'z'=8,'x'=4,'yl'=2,'core'=2] {'core','x','yl'}, dimensions={0} | all-to-all | bytes 786432 | tf_op jit(solution)/shard_map/all_to_all | solution.py:52
  69.9 0.2 exponential_reduce_fusion
  70.1 0.1 select_multiply_fusion
  70.3 0.1 fusion.38
  70.5 0.1 slice_add_fusion
  70.6 0.0 copy-done
  70.6 1.9 %fusion.5 = (f32[1024]{0:T(1024)S(1)}, f32[384,1024]{0,1:T(8,128)S(1)}) fusion(f32[512,1024]{1,0:T(8,128)S(1)} %copy-done, f32[512,256]{1,0:T(8,128)S(1)} %slice.144, f32[512,128]{1,0:T(8,128)S(1)} %slice_add_fusion), kind=kOutput, calls=%fused_computation.17 | convolution fusion | flops 1208941568 | bytes 4460544 | tf_op jit(solution)/shard_map/dot_general | solution.py:188
  72.6 1.1 %fusion.4 = f16[1024,384]{1,0:T(8,128)(2,1)S(1)} fusion(f32[384,1024]{0,1:T(8,128)S(1)} %get-tuple-element.44, f32[1024]{0:T(1024)S(1)} %get-tuple-element.29, f32[1024]{0:T(1024)S(1)} %get-tuple-element.28, pred[384]{0:T(512)(128)(4,1)S(1)} %get-tuple-element.46, pred[384]{0:T(512)(128)(4,1)S(1)} %get-tuple-element.45), kind=kLoop, calls=%fused_computation.14 | loop fusion | flops 2359296 | bytes 2368256 | tf_op jit(solution)/shard_map/convert_element_type | solution.py:70
  73.7 31.0 %all_to_all.31 = f16[32,32,384]{2,1,0:T(8,128)(2,1)S(1)} all-to-all(f16[32,32,384]{2,1,0:T(8,128)(2,1)S(1)} %bitcast.39), channel_id=1, replica_groups=mesh['yh'=4,'z'=8,'x'=4,'yl'=2,'core'=2] {'yh','z'}, dimensions={0} | all-to-all | bytes 1572864 | tf_op jit(solution)/shard_map/all_to_all | solution.py:52
  104.6 0.2 slice.145
  104.9 0.3 copy.28
  105.1 0.0 copy-start.3
  105.1 0.2 multiply_reduce_fusion
  105.4 0.9 copy-done.3
  106.3 0.9 fusion.40
  (34 shorter events, 0.4 us)
Async XLA Ops:
  0.0 70.6 %copy-start = (f32[512,1024]{1,0:T(8,128)S(1)}, f32[512,1024]{1,0:T(8,128)}, u32[]{:S(2)}) copy-start(f32[512,1024]{1,0:T(8,128)} %param.16) | copy-start | bytes 6291460
  0.0 17.6 %copy-start.2 = (bf16[512,128]{1,0:T(8,128)(2,1)S(1)}, bf16[512,128]{1,0:T(8,128)(2,1)}, u32[]{:S(2)}) copy-start(bf16[512,128]{1,0:T(8,128)(2,1)} %occ_ref.1) | copy-start | bytes 393220
  0.0 17.6 %copy-start.1 = (bf16[512,512]{1,0:T(8,128)(2,1)S(1)}, bf16[512,512]{1,0:T(8,128)(2,1)}, u32[]{:S(2)}) copy-start(bf16[512,512]{1,0:T(8,128)(2,1)} %vir_ref.1) | copy-start | bytes 1572868
  0.0 17.7 %copy-start.8 = (f32[128]{0:T(128)S(1)}, f32[128]{0:T(128)}, u32[]{:S(2)}) copy-start(f32[128]{0:T(128)} %param.14) | copy-start | bytes 1540
  0.0 17.7 %copy-start.5 = (f32[512]{0:T(512)S(1)}, f32[512]{0:T(512)}, u32[]{:S(2)}) copy-start(f32[512]{0:T(512)} %param.15) | copy-start | bytes 6148
  2.4 17.3 %copy-start.7 = (s32[32]{0:T(128)S(1)}, s32[32]{0:T(128)}, u32[]{:S(2)}) copy-start(s32[32]{0:T(128)} %cols_ref.1) | copy-start | bytes 388
  2.4 17.4 %copy-start.6 = (pred[32,32]{1,0:T(32,128)(4,1)S(1)}, pred[32,32]{1,0:T(32,128)(4,1)}, u32[]{:S(2)}) copy-start(pred[32,32]{1,0:T(32,128)(4,1)} %constant.97.clone) | copy-start | bytes 3076
  2.4 29.9 %all-to-all-start.2 = ((bf16[32,8,640]{2,1,0:T(8,128)(2,1)}), bf16[32,8,640]{2,1,0:T(8,128)(2,1)S(1)}, u32[]{:S(2)}, u32[]{:S(2)}) async-start(bf16[32,8,640]{2,1,0:T(8,128)(2,1)} %shard_map.91), calls=%async_computation.2 | async-start | bytes 655360 | tf_op jit(solution)/shard_map/all_to_all | solution.py:52
  17.8 3.7 %collective-permute-start = (bf16[264,640]{1,0:T(8,128)(2,1)S(1)}, bf16[264,640]{1,0:T(8,128)(2,1)}, u32[]{:S(2)}, u32[]{:S(2)}) collective-permute-start(bf16[264,640]{1,0:T(8,128)(2,1)S(1)} %pad_maximum_fusion.1), channel_id=1, source_target_pairs={{0,1},{1,0},{2,3},{3,2},{4,5},{5,4},{6,7},{7,6},{8,9},{9,8},{10,11... | collective-permute-start | bytes 1013768 | tf_op jit(solution)/shard_map/ppermute | solution.py:140
  32.6 3.2 %collective-permute-start.1 = (bf16[32,640]{1,0:T(8,128)(2,1)S(1)}, bf16[32,640]{1,0:T(8,128)(2,1)S(1)}, u32[]{:S(2)}, u32[]{:S(2)}) collective-permute-start(bf16[32,640]{1,0:T(8,128)(2,1)S(1)} %convert_element_type.101), channel_id=1, source_target_pairs={{0,1},{1,0},{2,3},{3,2},{4,5},{5,4},{6,7},{7,6},{8,9},{9,8},{10,11... | collective-permute-start | bytes 122888 | tf_op jit(solution)/shard_map/ppermute | solution.py:140
  40.0 16.7 %all-to-all-start.3 = ((f16[8,32,1152]{2,1,0:T(8,128)(2,1)}), f16[8,32,1152]{2,1,0:T(8,128)(2,1)S(1)}, u32[]{:S(2)}, u32[]{:S(2)}) async-start(f16[8,32,1152]{2,1,0:T(8,128)(2,1)} %bitcast.9), calls=%async_computation.3 | async-start | bytes 1179648 | tf_op jit(solution)/shard_map/all_to_all | solution.py:52
  46.4 11.0 %copy-start.4 = (f32[512,384]{1,0:T(8,128)S(1)}, f32[512,384]{1,0:T(8,128)}, u32[]{:S(2)}) copy-start(f32[512,384]{1,0:T(8,128)} %constant.98.clone) | copy-start | bytes 2359300
  105.1 1.1 %copy-start.3 = (f32[384,512]{1,0:T(8,128)S(1)}, f32[384,512]{1,0:T(8,128)}, u32[]{:S(2)}) copy-start(f32[384,512]{1,0:T(8,128)} %constant.99.clone) | copy-start | bytes 2359300

commit v5 on v4

--- a/solution.py
+++ b/solution.py
@@ -46,6 +46,7 @@
 
 
 LEFT, RIGHT = factors()
+MOMENTS = [float(m) for m in np.float32(0.05) * np.exp(np.float32(0.3) * np.arange(NT, dtype=np.float32))]
 
 
 def moved(x, axes):
@@ -100,6 +101,51 @@
     return with_layout_constraint(x, Layout(tuple(range(x.ndim))))
 
 
+def on_chip(body, shape, dtype, *args, scratch=()):
+    space = pl.BlockSpec(memory_space=pltpu.VMEM)
+    return pl.pallas_call(
+        body,
+        out_shape=pltpu.VMEM(shape, dtype),
+        in_specs=[space] * len(args),
+        out_specs=space,
+        scratch_shapes=scratch,
+    )(*[pltpu.with_memory_space_constraint(a, pltpu.VMEM) for a in args])
+
+
+def green_part(panel, occ_energy, vir_energy, occ, vir, scaled_ref):
+    no = occ.shape[1]
+    for energy, at in ((occ_energy, slice(0, no)), (vir_energy, slice(no, None))):
+        for t in range(NT):
+            decay = jnp.exp(-energy * MOMENTS[t])
+            scaled_ref[t * NC : (t + 1) * NC, at] = (panel[:, at] * decay).astype(bf16)
+    flipped = (((1,), (1,)), ((), ()))
+    return (
+        lax.dot_general(occ, scaled_ref[:, :no], flipped, preferred_element_type=f32),
+        lax.dot_general(vir, scaled_ref[:, no:], flipped, preferred_element_type=f32),
+    )
+
+
+def green_body(panel_ref, other_panel_ref, occ_e_ref, vir_e_ref, other_e_ref, occ_ref, vir_ref, theirs_ref, out_ref, scaled_ref):
+    times, no = NT * NC, occ_ref.shape[1]
+    half = occ_ref.shape[0]
+    occ, vir = green_part(panel_ref[...], occ_e_ref[...], vir_e_ref[...], occ_ref[...], vir_ref[...], scaled_ref.at[0])
+    energy, theirs = other_e_ref[...], theirs_ref[:half]
+    other_occ, other_vir = green_part(
+        other_panel_ref[...].astype(f32),
+        energy[:, :no],
+        energy[:, no:],
+        theirs[:, :no],
+        theirs[:, no:],
+        scaled_ref.at[1],
+    )
+    occ, vir = occ + other_occ, vir + other_vir
+    power = jnp.maximum(power_of(occ), power_of(vir))
+    factor = jnp.exp2(-power)
+    out_ref[:, :times] = occ * factor
+    out_ref[:, times : 2 * times] = vir * factor
+    out_ref[:, 2 * times :] = jnp.broadcast_to(power, (occ.shape[0], 128))
+
+
 def panel_rows(panel_cols, occ_orbitals, vir_orbitals):
     points, no = occ_orbitals.shape
     width = no + vir_orbitals.shape[1]
@@ -141,7 +187,6 @@
 
 
 def local(panel_cols, occ_orbitals, vir_orbitals, occ_energy, vir_energy, coulomb):
-    moments = 0.05 * jnp.exp(0.3 * jnp.arange(NT, dtype=f32))
     points, no = occ_orbitals.shape
     half = points // 2
     times = NT * NC
@@ -152,33 +197,33 @@
 
     panel, picked = panel_rows(panel_cols, occ_orbitals, vir_orbitals)
     occ_late, vir_late, _ = lax.optimization_barrier((occ_orbitals, vir_orbitals, picked))
+    right = lax.optimization_barrier(RIGHT + 0.0 * picked[0, 0, 0].astype(f32))
     energies = in_three(jnp.concatenate([occ_energy, vir_energy]))
     theirs = jnp.concatenate([rows_of(occ_late, 1 - core), rows_of(vir_late, 1 - core)], axis=1)
     theirs = jnp.concatenate([theirs, jnp.pad(energies, ((0, 5), (0, 0)))], axis=0)
     theirs = to_other_core(theirs)
-    other_panel = to_other_core(panel.astype(bf16)).astype(f32)
     pieces = theirs[half : half + 3].astype(f32)
-    other_energy = pieces[0] + pieces[1] + pieces[2]
-    theirs = theirs[:half]
-
-    def green(orbitals, energy, panel, first):
-        decay = jnp.exp(-energy[None, :] * moments[:, None])
-        decay = jnp.pad(decay, ((first, 2 * NT + 4 - NT - first), (0, 0)))
-        scaled = (panel[None] * decay[:, None]).astype(bf16).reshape(2 * times + 128, -1)
-        return lax.dot_general(orbitals, scaled, (((1,), (1,)), ((), ())), preferred_element_type=f32)
-
-    both = green(rows_of(vir_orbitals, core), vir_energy, panel[:, no:], NT)
-    both += green(rows_of(occ_orbitals, core), occ_energy, panel[:, :no], 0)
-    both += green(theirs[:, no:], other_energy[no:], other_panel[:, no:], NT)
-    both += green(theirs[:, :no], other_energy[:no], other_panel[:, :no], 0)
-    both = plain(both)
-    power = power_of(both)
-    sent = jnp.where(lanes(both) == 2 * times, power, both * jnp.exp2(-power)).astype(f16)
+    other_energy = pieces[0:1] + pieces[1:2] + pieces[2:3]
+    other_panel = to_other_core(panel.astype(bf16))
+    sent = on_chip(
+        green_body,
+        (half, 2 * times + 128),
+        f32,
+        panel,
+        other_panel,
+        occ_energy.reshape(1, -1),
+        vir_energy.reshape(1, -1),
+        other_energy,
+        rows_of(occ_late, core),
+        rows_of(vir_late, core),
+        theirs,
+        scratch=[pltpu.VMEM((2, times, panel.shape[1]), bf16)],
+    ).astype(f16)
     peers = lax.axis_size(("x", "yl"))
     got = moved(sent.reshape(peers, half // peers, -1), ("x", "yl"))
     power = got[..., 2 * times : 2 * times + 1].astype(f32)
     both = (got.astype(f32) * jnp.exp2(power)).sum(axis=0)
-    product = both[:, :times] * both[:, times : 2 * times]
+    product, right = lax.optimization_barrier((both[:, :times] * both[:, times : 2 * times], right))
     polar = packed(jnp.dot(product, LEFT, precision=HIGH, preferred_element_type=f32))
     polar = moved(jnp.broadcast_to(polar, (lax.axis_size(ORB), *polar.shape)), ("core", "x", "yl"))
     polar = unpacked(polar.reshape(points, WIDTH))
@@ -188,7 +233,7 @@
     part = lax.dot_general(coulomb, polar, (((0,), (0,)), ((), ())), precision=HIGH, preferred_element_type=f32)
     blocks = moved(packed(plain(part)).reshape(NC, -1, WIDTH), YZ)
     total = unpacked(blocks).sum(axis=0)
-    return jnp.dot(total, RIGHT, precision=HIGH, preferred_element_type=f32)
+    return jnp.dot(total, right, precision=HIGH, preferred_element_type=f32)
 
 
 def solution(mesh):

time: 108 us -> 105 us (0.972)
  matrix products: 7.18 us -> 3.58 us
  other arithmetic: 5.93 us -> 4.25 us
  local copies, waits for them, and re-layouts: 2.03 us -> 3.56 us
    dot_general x5 -> x1, matrix products: 4.54 us -> 0.96 us  [local(): return jnp.dot(total, right, precision=HIGH, preferred_element_type=f32)]
    all_to_all x2, waiting for transfers between devices: 20.2 us -> 19 us  [moved(): return lax.all_to_all(x, axes, split_axis=0, concat_axis=0, tiled=True)]
    slice x5 -> x2, local copies, waits for them, and re-layouts: 0.03 us -> 1.19 us  [the longest x1 1.18 us: local(): right = lax.optimization_barrier(RIGHT + 0.0 * picked[0, 0, 0].astype(f32))]
  transfers between devices with their start and end apart: 4 -> 4, of which waited for: 3 -> 4; matrix products, arithmetic and copies ran while one was open for 3% -> 2% of each run, Pallas kernels for 0% -> 0%
where the time goes in v5:
time: 105 us; the launch traced here: 104 us
  blocking collectives  42.7 us (41%)
  starting transfers between devices  25.5 us (24%)
  waiting for transfers between devices  20.2 us (19%)
  other arithmetic  4.25 us (4%)
  matrix products  3.58 us (3%)
  local copies, waits for them, and re-layouts  3.56 us (3%)
  Pallas kernels  2.98 us (3%)
  between operations  1.66 us (2%)
    all_to_all x2, blocking collectives, moved(): return lax.all_to_all(x, axes, split_axis=0, concat_axis=0, tiled=True)  42.7 us
    all_to_all x2, starting transfers between devices, moved(): return lax.all_to_all(x, axes, split_axis=0, concat_axis=0, tiled=True)  21.6 us
    all_to_all x2, waiting for transfers between devices, moved(): return lax.all_to_all(x, axes, split_axis=0, concat_axis=0, tiled=True)  19 us
    ppermute x2, starting transfers between devices, to_other_core(): return lax.ppermute(x, 'core', [(0, 1), (1, 0)])  3.84 us
    pallas_call x1, Pallas kernels, panel_rows(): pl.pallas_call(pick_body, out_shape=jax.ShapeDtypeStruct((blocks, SLOTS,...  2.24 us
  transfers between devices with their start and end apart: 4, of which 4 were waited for; matrix products, arithmetic and copies ran while one was open for 2% of the time, Pallas kernels for 0%

profile of v5, /device:TPU:8, one launch (start us, length us, event | category | flops | bytes accessed | tf_op | source)
XLA Modules:
  0.0 104.5 jit_solution(1123809769523810717)
XLA Ops:
  0.0 0.0 copy-start.2
  0.0 0.0 copy-start.6
  0.0 0.0 copy-start
  0.0 0.0 copy-start.1
  0.0 2.2 %shard_map.91 = bf16[32,8,640]{2,1,0:T(8,128)(2,1)} custom-call(s32[32]{0:T(128)} %cols_ref.1, bf16[512,128]{1,0:T(8,128)(2,1)} %occ_ref.1, bf16[512,512]{1,0:T(8,128)(2,1)} %vir_ref.1), custom_call_target="tpu_custom_call" | custom-call | tf_op jit(solution)/shard_map/pallas_call | solution.py:153
  2.3 0.0 copy-start.8
  2.3 0.0 copy-start.7
  2.3 15.2 %all-to-all-start.2 = ((bf16[32,8,640]{2,1,0:T(8,128)(2,1)}), bf16[32,8,640]{2,1,0:T(8,128)(2,1)S(1)}, u32[]{:S(2)}, u32[]{:S(2)}) async-start(bf16[32,8,640]{2,1,0:T(8,128)(2,1)} %shard_map.91), calls=%async_computation.2 | async-start | bytes 655360 | tf_op jit(solution)/shard_map/all_to_all | solution.py:53
  17.5 0.0 copy-done.6
  17.5 0.0 copy-done.2
  17.6 0.0 copy-done
  17.6 0.0 copy-done.1
  17.7 1.9 %collective-permute-start.1 = (bf16[264,640]{1,0:T(8,128)(2,1)S(1)}, bf16[264,640]{1,0:T(8,128)(2,1)S(1)}, u32[]{:S(2)}, u32[]{:S(2)}) collective-permute-start(bf16[264,640]{1,0:T(8,128)(2,1)S(1)} %pad_maximum_fusion.1), channel_id=1, source_target_pairs={{0,1},{1,0},{2,3},{3,2},{4,5},{5,4},{6,7},{7,6},{8,9},{9,8},{10,11... | collective-permute-start | bytes 1013768 | tf_op jit(solution)/shard_map/ppermute | solution.py:186
  19.6 0.0 copy-done.8
  19.6 0.0 copy-done.7
  19.7 0.2 convert_reduce_fusion
  19.8 0.6 compare_reduce_fusion
  21.1 0.1 collective-permute-done.1.theirs_ref
  21.2 11.0 %all-to-all-done.2 = bf16[32,8,640]{2,1,0:T(8,128)(2,1)S(1)} async-done(((bf16[32,8,640]{2,1,0:T(8,128)(2,1)}), bf16[32,8,640]{2,1,0:T(8,128)(2,1)S(1)}, u32[]{:S(2)}, u32[]{:S(2)}) %all-to-all-start.2) | async-done | bytes 327712 | tf_op jit(solution)/shard_map/all_to_all | solution.py:53
  32.2 0.2 fusion.9
  32.4 1.9 %collective-permute-start = (bf16[32,640]{1,0:T(8,128)(2,1)S(1)}, bf16[32,640]{1,0:T(8,128)(2,1)S(1)}, u32[]{:S(2)}, u32[]{:S(2)}) collective-permute-start(bf16[32,640]{1,0:T(8,128)(2,1)S(1)} %convert_element_type.64), channel_id=1, source_target_pairs={{0,1},{1,0},{2,3},{3,2},{4,5},{5,4},{6,7},{7,6},{8,9},{9,8},{10,11... | collective-permute-start | bytes 122888 | tf_op jit(solution)/shard_map/ppermute | solution.py:186
  34.4 1.2 %collective-permute-done.other_panel_ref = bf16[32,640]{1,0:T(8,128)(2,1)S(1)} collective-permute-done((bf16[32,640]{1,0:T(8,128)(2,1)S(1)}, bf16[32,640]{1,0:T(8,128)(2,1)S(1)}, u32[]{:S(2)}, u32[]{:S(2)}) %collective-permute-start) | collective-permute-done | bytes 40992 | tf_op jit(solution)/shard_map/ppermute | solution.py:186
  35.6 0.7 shard_map.92
  36.3 0.0 copy-start.4
  36.3 0.9 convert_element_type.66
  37.2 6.4 %all-to-all-start.3 = ((f16[8,32,1152]{2,1,0:T(8,128)(2,1)}), f16[8,32,1152]{2,1,0:T(8,128)(2,1)S(1)}, u32[]{:S(2)}, u32[]{:S(2)}) async-start(f16[8,32,1152]{2,1,0:T(8,128)(2,1)} %bitcast.3), calls=%async_computation.3 | async-start | bytes 1179648 | tf_op jit(solution)/shard_map/all_to_all | solution.py:53
  43.6 1.2 %slice.87 = bf16[1,1,1]{2,1,0:T(2,128)(2,1)} slice(bf16[32,8,640]{2,1,0:T(8,128)(2,1)} %shard_map.91), slice={[0:1], [0:1], [0:1]} | slice | bytes 4 | tf_op jit(solution)/shard_map/slice | solution.py:200
  45.5 0.0 copy-done.4
  45.5 0.1 broadcast_add_fusion
  45.6 0.0 copy-start.5
  45.6 8.0 %all-to-all-done.3 = f16[8,32,1152]{2,1,0:T(8,128)(2,1)S(1)} async-done(((f16[8,32,1152]{2,1,0:T(8,128)(2,1)}), f16[8,32,1152]{2,1,0:T(8,128)(2,1)S(1)}, u32[]{:S(2)}, u32[]{:S(2)}) %all-to-all-start.3) | async-done | bytes 589856 | tf_op jit(solution)/shard_map/all_to_all | solution.py:53
  53.6 0.1 copy.25
  53.7 0.2 multiply_reduce_fusion.1
  54.0 0.1 copy.27
  54.1 0.1 copy.26
  54.3 0.0 copy-done.5
  54.3 0.5 abs_reduce_fusion
  54.8 0.1 fusion.12
  55.0 11.8 %all_to_all.30 = f16[16,32,384]{2,1,0:T(8,128)(2,1)S(1)} all-to-all(f16[16,32,384]{2,1,0:T(8,128)(2,1)S(1)} %broadcast_in_dim.39), channel_id=1, replica_groups=mesh['yh'=4,'z'=8,'x'=4,'yl'=2,'core'=2] {'core','x','yl'}, dimensions={0} | all-to-all | bytes 786432 | tf_op jit(solution)/shard_map/all_to_all | solution.py:53
  66.8 0.2 exponential_reduce_fusion
  67.1 0.1 select_multiply_fusion
  67.2 0.0 copy-start.3
  67.3 0.1 fusion.22
  67.4 0.1 slice_add_fusion
  67.6 1.3 %copy-done.3 = f32[512,1024]{1,0:T(8,128)S(1)} copy-done((f32[512,1024]{1,0:T(8,128)S(1)}, f32[512,1024]{1,0:T(8,128)}, u32[]{:S(2)}) %copy-start.3) | copy-done | bytes 2097176
  68.8 1.9 %fusion.4 = (f32[1024]{0:T(1024)S(1)}, f32[384,1024]{0,1:T(8,128)S(1)}) fusion(f32[512,1024]{1,0:T(8,128)S(1)} %copy-done.3, f32[512,256]{1,0:T(8,128)S(1)} %slice.92, f32[512,128]{1,0:T(8,128)S(1)} %slice_add_fusion), kind=kOutput, calls=%fused_computation.12 | convolution fusion | flops 1208941568 | bytes 4460544 | tf_op jit(solution)/shard_map/dot_general | solution.py:233
  70.7 1.1 %fusion.3 = f16[1024,384]{1,0:T(8,128)(2,1)S(1)} fusion(f32[384,1024]{0,1:T(8,128)S(1)} %get-tuple-element.44, f32[1024]{0:T(1024)S(1)} %get-tuple-element.37, f32[1024]{0:T(1024)S(1)} %get-tuple-element.36, pred[384]{0:T(512)(128)(4,1)S(1)} %get-tuple-element.46, pred[384]{0:T(512)(128)(4,1)S(1)} %get-tuple-element.45), kind=kLoop, calls=%fused_computation.9 | loop fusion | flops 2359296 | bytes 2368256 | tf_op jit(solution)/shard_map/convert_element_type | solution.py:71
  71.8 30.9 %all_to_all.31 = f16[32,32,384]{2,1,0:T(8,128)(2,1)S(1)} all-to-all(f16[32,32,384]{2,1,0:T(8,128)(2,1)S(1)} %bitcast.32), channel_id=1, replica_groups=mesh['yh'=4,'z'=8,'x'=4,'yl'=2,'core'=2] {'yh','z'}, dimensions={0} | all-to-all | bytes 1572864 | tf_op jit(solution)/shard_map/all_to_all | solution.py:53
  102.8 0.2 slice.93
  103.0 0.3 copy.28
  103.3 0.2 multiply_reduce_fusion
  103.5 1.0 fusion.24
  (21 shorter events, 0.4 us)
Async XLA Ops:
  0.0 17.5 %copy-start.2 = (bf16[512,512]{1,0:T(8,128)(2,1)S(1)}, bf16[512,512]{1,0:T(8,128)(2,1)}, u32[]{:S(2)}) copy-start(bf16[512,512]{1,0:T(8,128)(2,1)} %vir_ref.1) | copy-start | bytes 1572868
  0.0 17.5 %copy-start.6 = (bf16[512,128]{1,0:T(8,128)(2,1)S(1)}, bf16[512,128]{1,0:T(8,128)(2,1)}, u32[]{:S(2)}) copy-start(bf16[512,128]{1,0:T(8,128)(2,1)} %occ_ref.1) | copy-start | bytes 393220
  0.0 17.6 %copy-start = (f32[512]{0:T(512)S(1)}, f32[512]{0:T(512)}, u32[]{:S(2)}) copy-start(f32[512]{0:T(512)} %param.15) | copy-start | bytes 6148
  0.0 17.6 %copy-start.1 = (f32[128]{0:T(128)S(1)}, f32[128]{0:T(128)}, u32[]{:S(2)}) copy-start(f32[128]{0:T(128)} %param.14) | copy-start | bytes 1540
  2.3 17.4 %copy-start.8 = (s32[32]{0:T(128)S(1)}, s32[32]{0:T(128)}, u32[]{:S(2)}) copy-start(s32[32]{0:T(128)} %cols_ref.1) | copy-start | bytes 388
  2.3 17.4 %copy-start.7 = (pred[32,32]{1,0:T(32,128)(4,1)S(1)}, pred[32,32]{1,0:T(32,128)(4,1)}, u32[]{:S(2)}) copy-start(pred[32,32]{1,0:T(32,128)(4,1)} %constant.87.clone) | copy-start | bytes 3076
  2.3 29.9 %all-to-all-start.2 = ((bf16[32,8,640]{2,1,0:T(8,128)(2,1)}), bf16[32,8,640]{2,1,0:T(8,128)(2,1)S(1)}, u32[]{:S(2)}, u32[]{:S(2)}) async-start(bf16[32,8,640]{2,1,0:T(8,128)(2,1)} %shard_map.91), calls=%async_computation.2 | async-start | bytes 655360 | tf_op jit(solution)/shard_map/all_to_all | solution.py:53
  17.7 3.5 %collective-permute-start.1 = (bf16[264,640]{1,0:T(8,128)(2,1)S(1)}, bf16[264,640]{1,0:T(8,128)(2,1)S(1)}, u32[]{:S(2)}, u32[]{:S(2)}) collective-permute-start(bf16[264,640]{1,0:T(8,128)(2,1)S(1)} %pad_maximum_fusion.1), channel_id=1, source_target_pairs={{0,1},{1,0},{2,3},{3,2},{4,5},{5,4},{6,7},{7,6},{8,9},{9,8},{10,11... | collective-permute-start | bytes 1013768 | tf_op jit(solution)/shard_map/ppermute | solution.py:186
  32.4 3.1 %collective-permute-start = (bf16[32,640]{1,0:T(8,128)(2,1)S(1)}, bf16[32,640]{1,0:T(8,128)(2,1)S(1)}, u32[]{:S(2)}, u32[]{:S(2)}) collective-permute-start(bf16[32,640]{1,0:T(8,128)(2,1)S(1)} %convert_element_type.64), channel_id=1, source_target_pairs={{0,1},{1,0},{2,3},{3,2},{4,5},{5,4},{6,7},{7,6},{8,9},{9,8},{10,11... | collective-permute-start | bytes 122888 | tf_op jit(solution)/shard_map/ppermute | solution.py:186
  36.3 9.2 %copy-start.4 = (f32[384,512]{1,0:T(8,128)S(1)}, f32[384,512]{1,0:T(8,128)}, u32[]{:S(2)}) copy-start(f32[384,512]{1,0:T(8,128)} %constant.88.clone) | copy-start | bytes 2359300
  37.2 16.4 %all-to-all-start.3 = ((f16[8,32,1152]{2,1,0:T(8,128)(2,1)}), f16[8,32,1152]{2,1,0:T(8,128)(2,1)S(1)}, u32[]{:S(2)}, u32[]{:S(2)}) async-start(f16[8,32,1152]{2,1,0:T(8,128)(2,1)} %bitcast.3), calls=%async_computation.3 | async-start | bytes 1179648 | tf_op jit(solution)/shard_map/all_to_all | solution.py:53
  45.6 8.8 %copy-start.5 = (f32[512,384]{1,0:T(8,128)S(1)}, f32[512,384]{1,0:T(8,128)}, u32[]{:S(2)}) copy-start(f32[512,384]{1,0:T(8,128)} %constant.89.clone) | copy-start | bytes 2359300
  67.2 1.6 %copy-start.3 = (f32[512,1024]{1,0:T(8,128)S(1)}, f32[512,1024]{1,0:T(8,128)}, u32[]{:S(2)}) copy-start(f32[512,1024]{1,0:T(8,128)} %param.16) | copy-start | bytes 6291460

commit v6 on v5

--- a/solution.py
+++ b/solution.py
@@ -3,7 +3,6 @@
 import numpy as np
 from jax import lax
 from jax.experimental import pallas as pl
-from jax.experimental.layout import Layout, with_layout_constraint
 from jax.experimental.pallas import tpu as pltpu
 from jax.sharding import Mesh
 from jax.sharding import PartitionSpec as P
@@ -16,9 +15,9 @@
 WIDTH = 384
 SPARE = 127
 SLOTS = 8
+VMEM_LIMIT = 12 * 2**20
 YZ = ("yh", "z")
 ORB = ("x", "yl", "core")
-HIGH = lax.Precision.HIGH
 f32, f16, bf16 = jnp.float32, jnp.float16, jnp.bfloat16
 
 
@@ -33,19 +32,10 @@
     up = u @ turn
     down = up.T @ table
     slots = [*range(TWICE), *range(TWICE), *range(TWICE, RANK)]
-    left = np.zeros((NT, NC, len(slots), NC))
-    right = np.zeros((len(slots), NC, NC, NF))
-    for k, j in enumerate(slots):
-        for c in range(NC):
-            left[:, c, k, c] = down[j]
-            right[k, c, c, :] = up[:, j]
-    return (
-        left.reshape(NT * NC, WIDTH).astype(np.float32),
-        right.reshape(WIDTH, NC * NF).astype(np.float32),
-    )
-
-
-LEFT, RIGHT = factors()
+    return np.repeat(down[slots].T, NC, axis=1).astype(np.float32), np.tile(up[:, slots].T, (1, NC)).astype(np.float32)
+
+
+DOWN, UP = factors()
 MOMENTS = [float(m) for m in np.float32(0.05) * np.exp(np.float32(0.3) * np.arange(NT, dtype=np.float32))]
 
 
@@ -62,19 +52,31 @@
     return lax.broadcasted_iota(jnp.int32, x.shape, x.ndim - 1)
 
 
-def packed(x):
+def spread(x):
     power = power_of(x)
     scaled = x * jnp.exp2(-power)
+    wide = scaled * 8193.0
+    high = wide - (wide - scaled)
     lane = lanes(x)
-    rest = scaled - lax.reduce_precision(scaled, 5, 10)
-    low = (lane >= 64) & (lane < 128)
-    return jnp.where(lane == SPARE, power, jnp.where(low, rest, scaled)).astype(f16)
+    scaled = jnp.where(lane < 64, high, jnp.where(lane < 128, scaled - high, scaled))
+    return jnp.where(lane == SPARE, power, scaled)
 
 
 def unpacked(y):
-    power = y[..., SPARE : SPARE + 1].astype(f32)
-    y = y.astype(f32)
+    power = y[:, SPARE : SPARE + 1]
     return jnp.where(lanes(y) == SPARE, 0.0, y) * jnp.exp2(power)
+
+
+def two_parts(x):
+    high = x.astype(bf16)
+    return high, (x - high.astype(f32)).astype(bf16)
+
+
+def product_of(x, y):
+    (a, b), (c, d) = x, y
+    total = jnp.dot(a, c, preferred_element_type=f32)
+    total += jnp.dot(a, d, preferred_element_type=f32)
+    return total + jnp.dot(b, c, preferred_element_type=f32)
 
 
 def pick_body(cols_ref, occ_ref, vir_ref, out_ref):
@@ -97,19 +99,16 @@
         out_ref[k, :, no:] = vir
 
 
-def plain(x):
-    return with_layout_constraint(x, Layout(tuple(range(x.ndim))))
-
-
-def on_chip(body, shape, dtype, *args, scratch=()):
+def on_chip(body, shape, dtype, *args, scratch=(), last=False):
     space = pl.BlockSpec(memory_space=pltpu.VMEM)
     return pl.pallas_call(
         body,
-        out_shape=pltpu.VMEM(shape, dtype),
+        out_shape=jax.ShapeDtypeStruct(shape, dtype) if last else pltpu.VMEM(shape, dtype),
         in_specs=[space] * len(args),
         out_specs=space,
         scratch_shapes=scratch,
-    )(*[pltpu.with_memory_space_constraint(a, pltpu.VMEM) for a in args])
+        compiler_params=pltpu.CompilerParams(vmem_limit_bytes=VMEM_LIMIT),
+    )(*[pltpu.with_memory_space_constraint(jnp.asarray(a), pltpu.VMEM) for a in args])
 
 
 def green_part(panel, occ_energy, vir_energy, occ, vir, scaled_ref):
@@ -146,6 +145,41 @@
     out_ref[:, 2 * times :] = jnp.broadcast_to(power, (occ.shape[0], 128))
 
 
+def polar_body(got_ref, down_ref, out_ref, table_ref):
+    times = NT * NC
+    occ, vir = 0.0, 0.0
+    for k in range(got_ref.shape[0]):
+        factor = jnp.exp2(got_ref[k, :, 2 * times : 2 * times + 1])
+        occ += got_ref[k, :, :times] * factor
+        vir += got_ref[k, :, times : 2 * times] * factor
+    column = lax.broadcasted_iota(jnp.int32, (NC, WIDTH), 0)
+    same = (column == lax.broadcasted_iota(jnp.int32, (NC, WIDTH), 1) % NC).astype(f32)
+    for t in range(NT):
+        table_ref[t * NC : (t + 1) * NC, :] = same * down_ref[t : t + 1, :]
+    out_ref[...] = spread(product_of(two_parts(occ * vir), two_parts(table_ref[...])))
+
+
+def screen_body(coulomb_ref, polar_ref, out_ref):
+    polar = unpacked(polar_ref[...])
+    pair = polar[:, :128]
+    polar = two_parts(jnp.concatenate([pair + pltpu.roll(pair, 64, 1), polar[:, 128:]], axis=1))
+    step = 256
+    for at in range(0, out_ref.shape[0], step):
+        block = two_parts(coulomb_ref[:, at : at + step].T)
+        out_ref[at : at + step, :] = spread(product_of(block, polar))
+
+
+def total_body(blocks_ref, up_ref, out_ref, table_ref):
+    total = 0.0
+    for k in range(blocks_ref.shape[0]):
+        total += unpacked(blocks_ref[k])
+    column = lax.broadcasted_iota(jnp.int32, (NC, NC * NF), 0)
+    same = (column == lax.broadcasted_iota(jnp.int32, (NC, NC * NF), 1) // NF).astype(f32)
+    for k in range(WIDTH // NC):
+        table_ref[k * NC : (k + 1) * NC, :] = same * up_ref[k : k + 1, :]
+    out_ref[...] = product_of(two_parts(total), two_parts(table_ref[...]))
+
+
 def panel_rows(panel_cols, occ_orbitals, vir_orbitals):
     points, no = occ_orbitals.shape
     width = no + vir_orbitals.shape[1]
@@ -154,6 +188,7 @@
         pick_body,
         out_shape=jax.ShapeDtypeStruct((blocks, SLOTS, width), bf16),
         in_specs=[pl.BlockSpec(memory_space=pltpu.SMEM)] + [pl.BlockSpec(memory_space=pltpu.VMEM)] * 2,
+        compiler_params=pltpu.CompilerParams(vmem_limit_bytes=VMEM_LIMIT),
     )(panel_cols, occ_orbitals, vir_orbitals)
     got = moved(sent, YZ).reshape(blocks * SLOTS, width)
     block = panel_cols // points
@@ -197,7 +232,8 @@
 
     panel, picked = panel_rows(panel_cols, occ_orbitals, vir_orbitals)
     occ_late, vir_late, _ = lax.optimization_barrier((occ_orbitals, vir_orbitals, picked))
-    right = lax.optimization_barrier(RIGHT + 0.0 * picked[0, 0, 0].astype(f32))
+    coulomb = coulomb + 0.0 * picked[0, 0, 0].astype(f32)
+    panel, coulomb = lax.optimization_barrier((panel, coulomb))
     energies = in_three(jnp.concatenate([occ_energy, vir_energy]))
     theirs = jnp.concatenate([rows_of(occ_late, 1 - core), rows_of(vir_late, 1 - core)], axis=1)
     theirs = jnp.concatenate([theirs, jnp.pad(energies, ((0, 5), (0, 0)))], axis=0)
@@ -221,19 +257,14 @@
     ).astype(f16)
     peers = lax.axis_size(("x", "yl"))
     got = moved(sent.reshape(peers, half // peers, -1), ("x", "yl"))
-    power = got[..., 2 * times : 2 * times + 1].astype(f32)
-    both = (got.astype(f32) * jnp.exp2(power)).sum(axis=0)
-    product, right = lax.optimization_barrier((both[:, :times] * both[:, times : 2 * times], right))
-    polar = packed(jnp.dot(product, LEFT, precision=HIGH, preferred_element_type=f32))
+    table = [pltpu.VMEM((times, WIDTH), f32)]
+    polar = on_chip(polar_body, (got.shape[1], WIDTH), f32, got.astype(f32), DOWN, scratch=table).astype(f16)
     polar = moved(jnp.broadcast_to(polar, (lax.axis_size(ORB), *polar.shape)), ("core", "x", "yl"))
-    polar = unpacked(polar.reshape(points, WIDTH))
-    pair = polar[:, :128]
-    pair = pair + jnp.roll(pair, 64, axis=1)
-    polar = jnp.concatenate([pair, polar[:, 128:]], axis=1)
-    part = lax.dot_general(coulomb, polar, (((0,), (0,)), ((), ())), precision=HIGH, preferred_element_type=f32)
-    blocks = moved(packed(plain(part)).reshape(NC, -1, WIDTH), YZ)
-    total = unpacked(blocks).sum(axis=0)
-    return jnp.dot(total, right, precision=HIGH, preferred_element_type=f32)
+    polar = polar.reshape(points, WIDTH).astype(f32)
+    part = on_chip(screen_body, (coulomb.shape[1], WIDTH), f32, coulomb, polar).astype(f16)
+    blocks = moved(part.reshape(NC, -1, WIDTH), YZ).astype(f32)
+    table = [pltpu.VMEM((WIDTH, NC * NF), f32)]
+    return on_chip(total_body, (blocks.shape[1], NC * NF), f32, blocks, UP, scratch=table, last=True)
 
 
 def solution(mesh):

time: 105 us -> 102 us (0.971)
  blocking collectives: 42.7 us -> 59.8 us
  waiting for transfers between devices: 20.2 us -> 7.1 us
  starting transfers between devices: 25.5 us -> 19 us
  Pallas kernels: 2.98 us -> 6.89 us
  matrix products: 3.58 us -> 1.17 us
  local copies, waits for them, and re-layouts: 3.56 us -> 1.26 us
    all_to_all x2 -> x3, blocking collectives: 42.7 us -> 59.8 us  [moved(): return lax.all_to_all(x, axes, split_axis=0, concat_axis=0, tiled=True)]
    all_to_all x2 -> x1, waiting for transfers between devices: 19 us -> 5.92 us  [moved(): return lax.all_to_all(x, axes, split_axis=0, concat_axis=0, tiled=True)]
    all_to_all x2 -> x1, starting transfers between devices: 21.6 us -> 15.2 us  [moved(): return lax.all_to_all(x, axes, split_axis=0, concat_axis=0, tiled=True)]
    pallas_call x1 -> x4, Pallas kernels: 0.73 us -> 4.69 us  [on_chip(): pl.pallas_call(body, out_shape=jax.ShapeDtypeStruct(shape, dtype) if last...]
    dot_general x3 -> x0, matrix products: 3.39 us -> none  [the longest x1 1.92 us: local(): lax.dot_general(coulomb, polar, (((0,), (0,)), ((), ())), precision=HIGH,...]
    unnamed x22 -> x16, local copies, waits for them, and re-layouts: 1.94 us -> 0.04 us
    add x2 -> x1, other arithmetic: 0.21 us -> 1.79 us  [local(): coulomb = coulomb + 0.0 * picked[0, 0, 0].astype(f32)]
  transfers between devices with their start and end apart: 4 -> 3, of which waited for: 4 -> 2; matrix products, arithmetic and copies ran while one was open for 2% -> 5% of each run, Pallas kernels for 0% -> 0%
where the time goes in v6:
time: 102 us
  blocking collectives  59.8 us (59%)
  starting transfers between devices  19 us (19%)
  waiting for transfers between devices  7.1 us (7%)
  Pallas kernels  6.89 us (7%)
  other arithmetic  4.91 us (5%)
  between operations  1.51 us (1%)
  local copies, waits for them, and re-layouts  1.26 us (1%)
  matrix products  1.17 us (1%)
    all_to_all x3, blocking collectives, moved(): return lax.all_to_all(x, axes, split_axis=0, concat_axis=0, tiled=True)  59.8 us
    all_to_all x1, starting transfers between devices, moved(): return lax.all_to_all(x, axes, split_axis=0, concat_axis=0, tiled=True)  15.2 us
    all_to_all x1, waiting for transfers between devices, moved(): return lax.all_to_all(x, axes, split_axis=0, concat_axis=0, tiled=True)  5.92 us
    pallas_call x4, Pallas kernels, on_chip(): pl.pallas_call(body, out_shape=jax.ShapeDtypeStruct(shape, dtype) if last...  4.69 us
    ppermute x2, starting transfers between devices, to_other_core(): return lax.ppermute(x, 'core', [(0, 1), (1, 0)])  3.83 us
    pallas_call x1, Pallas kernels, panel_rows(): pl.pallas_call(pick_body, out_shape=jax.ShapeDtypeStruct((blocks, SLOTS,...  2.2 us
  transfers between devices with their start and end apart: 3, of which 2 were waited for; matrix products, arithmetic and copies ran while one was open for 5% of the time, Pallas kernels for 0%

profile of v6, /device:TPU:8, one launch (start us, length us, event | category | flops | bytes accessed | tf_op | source)
XLA Modules:
  0.0 101.7 jit_solution(7587457619316749839)
XLA Ops:
  0.0 0.0 copy-start.6
  0.0 0.0 copy-start.7
  0.0 0.0 copy-start.4
  0.0 0.0 copy-start.2
  0.0 0.0 copy-start.3
  0.0 2.2 %shard_map.91 = bf16[32,8,640]{2,1,0:T(8,128)(2,1)} custom-call(s32[32]{0:T(128)} %cols_ref.1, bf16[512,128]{1,0:T(8,128)(2,1)} %occ_ref.1, bf16[512,512]{1,0:T(8,128)(2,1)} %vir_ref.1), custom_call_target="tpu_custom_call" | custom-call | tf_op jit(solution)/shard_map/pallas_call | solution.py:187
  2.2 15.2 %all-to-all-start.2 = ((bf16[32,8,640]{2,1,0:T(8,128)(2,1)}), bf16[32,8,640]{2,1,0:T(8,128)(2,1)}, u32[]{:S(2)}, u32[]{:S(2)}) async-start(bf16[32,8,640]{2,1,0:T(8,128)(2,1)} %shard_map.91), calls=%async_computation.2 | async-start | bytes 655360 | tf_op jit(solution)/shard_map/all_to_all | solution.py:43
  17.4 0.9 broadcast_select_fusion.2
  18.3 0.0 copy-done.4
  18.4 0.0 copy-done.2
  18.4 0.0 copy-done.3
  18.4 0.8 pad_maximum_fusion.1
  19.2 1.9 %collective-permute-start.1 = (bf16[264,640]{1,0:T(8,128)(2,1)}, bf16[264,640]{1,0:T(8,128)(2,1)S(1)}, u32[]{:S(2)}, u32[]{:S(2)}) collective-permute-start(bf16[264,640]{1,0:T(8,128)(2,1)} %pad_maximum_fusion.1), channel_id=1, source_target_pairs={{0,1},{1,0},{2,3},{3,2},{4,5},{5,4},{6,7},{7,6},{8,9},{9,8},{10,11... | collective-permute-start | bytes 1013768 | tf_op jit(solution)/shard_map/ppermute | solution.py:221
  21.1 0.0 copy-done.7
  21.2 0.0 copy-done.6
  21.2 0.2 convert_reduce_fusion
  21.4 0.6 compare_reduce_fusion
  22.0 1.2 %slice.40 = bf16[1,1,1]{2,1,0:T(2,128)(2,1)} slice(bf16[32,8,640]{2,1,0:T(8,128)(2,1)} %shard_map.91), slice={[0:1], [0:1], [0:1]} | slice | bytes 4 | tf_op jit(solution)/shard_map/slice | solution.py:235
  24.4 0.0 copy-start.5
  24.4 1.8 %broadcast_add_fusion.coulomb_ref = f32[512,1024]{1,0:T(8,128)S(1)} fusion(f32[512,1024]{1,0:T(8,128)} %param.16, f32[]{:T(128)} %bitcast.1), kind=kLoop, calls=%fused_computation.7 | loop fusion | flops 524288 | bytes 4194308 | tf_op jit(solution)/shard_map/add | solution.py:235
  26.2 0.0 collective-permute-done.1.theirs_ref
  26.2 5.9 %all-to-all-done.2 = bf16[32,8,640]{2,1,0:T(8,128)(2,1)} async-done(((bf16[32,8,640]{2,1,0:T(8,128)(2,1)}), bf16[32,8,640]{2,1,0:T(8,128)(2,1)}, u32[]{:S(2)}, u32[]{:S(2)}) %all-to-all-start.2) | async-done | bytes 327712 | tf_op jit(solution)/shard_map/all_to_all | solution.py:43
  32.1 0.0 copy-done.5
  32.1 1.2 %fusion.2 = f32[32,640]{1,0:T(8,128)S(1)} fusion(bf16[32,8,640]{2,1,0:T(8,128)(2,1)} %all-to-all-done.2, s32[32]{0:T(128)S(1)} %multiply_add_fusion), kind=kOutput, calls=%fused_computation.10 | convolution fusion | flops 10493952 | bytes 409728 | tf_op jit(solution)/shard_map/dot_general | solution.py:199
  33.4 1.9 %collective-permute-start = (bf16[32,640]{1,0:T(8,128)(2,1)S(1)}, bf16[32,640]{1,0:T(8,128)(2,1)S(1)}, u32[]{:S(2)}, u32[]{:S(2)}) collective-permute-start(bf16[32,640]{1,0:T(8,128)(2,1)S(1)} %convert_element_type.58), channel_id=1, source_target_pairs={{0,1},{1,0},{2,3},{3,2},{4,5},{5,4},{6,7},{7,6},{8,9},{9,8},{10,11... | collective-permute-start | bytes 122888 | tf_op jit(solution)/shard_map/ppermute | solution.py:221
  35.3 1.2 %collective-permute-done.other_panel_ref = bf16[32,640]{1,0:T(8,128)(2,1)S(1)} collective-permute-done((bf16[32,640]{1,0:T(8,128)(2,1)S(1)}, bf16[32,640]{1,0:T(8,128)(2,1)S(1)}, u32[]{:S(2)}, u32[]{:S(2)}) %collective-permute-start) | collective-permute-done | bytes 40992 | tf_op jit(solution)/shard_map/ppermute | solution.py:221
  36.5 0.7 shard_map.92
  37.2 0.0 copy-start.1
  37.2 0.1 convert_element_type.60
  37.3 16.2 %all_to_all.30 = f16[8,32,1152]{2,1,0:T(8,128)(2,1)S(1)} all-to-all(f16[8,32,1152]{2,1,0:T(8,128)(2,1)S(1)} %bitcast.18), channel_id=1, replica_groups=mesh['yh'=4,'z'=8,'x'=4,'yl'=2,'core'=2] {'x','yl'}, dimensions={0} | all-to-all | bytes 1179648 | tf_op jit(solution)/shard_map/all_to_all | solution.py:43
  53.5 0.1 convert_element_type.61.got_ref
  53.6 0.0 copy-done.1
  53.6 0.5 shard_map.93
  54.2 11.9 %all_to_all.31 = f16[16,32,384]{2,1,0:T(8,128)(2,1)S(1)} all-to-all(f16[16,32,384]{2,1,0:T(8,128)(2,1)S(1)} %broadcast_in_dim.4), channel_id=1, replica_groups=mesh['yh'=4,'z'=8,'x'=4,'yl'=2,'core'=2] {'core','x','yl'}, dimensions={0} | all-to-all | bytes 786432 | tf_op jit(solution)/shard_map/all_to_all | solution.py:43
  66.0 0.1 bitcast_convert_fusion.polar_ref
  66.1 2.3 %shard_map.94 = f32[1024,384]{1,0:T(8,128)S(1)} custom-call(f32[512,1024]{1,0:T(8,128)S(1)} %broadcast_add_fusion.coulomb_ref, f32[512,384]{1,0:T(8,128)S(1)} %bitcast_convert_fusion.polar_ref), custom_call_target="tpu_custom_call" | custom-call | tf_op jit(solution)/shard_map/pallas_call | solution.py:104
  68.4 0.1 convert_element_type.65
  68.5 0.0 copy-start
  68.5 31.8 %all_to_all.32 = f16[32,32,384]{2,1,0:T(8,128)(2,1)S(1)} all-to-all(f16[32,32,384]{2,1,0:T(8,128)(2,1)S(1)} %bitcast.17), channel_id=1, replica_groups=mesh['yh'=4,'z'=8,'x'=4,'yl'=2,'core'=2] {'yh','z'}, dimensions={0} | all-to-all | bytes 1572864 | tf_op jit(solution)/shard_map/all_to_all | solution.py:43
  100.3 0.2 convert_element_type.66.blocks_ref
  100.5 0.0 copy-done
  100.5 1.2 %shard_map.95 = f32[32,512]{1,0:T(8,128)} custom-call(f32[32,32,384]{2,1,0:T(8,128)S(1)} %convert_element_type.66.blocks_ref, f32[12,512]{1,0:T(8,128)S(1)} %copy-done), custom_call_target="tpu_custom_call" | custom-call | tf_op jit(solution)/shard_map/pallas_call | solution.py:104
  (11 shorter events, 0.2 us)
Async XLA Ops:
  0.0 21.2 %copy-start.6 = (pred[32,32]{1,0:T(32,128)(4,1)S(1)}, pred[32,32]{1,0:T(32,128)(4,1)}, u32[]{:S(2)}) copy-start(pred[32,32]{1,0:T(32,128)(4,1)} %constant.56.clone) | copy-start | bytes 3076
  0.0 21.1 %copy-start.7 = (s32[32]{0:T(128)S(1)}, s32[32]{0:T(128)}, u32[]{:S(2)}) copy-start(s32[32]{0:T(128)} %cols_ref.1) | copy-start | bytes 388
  0.0 18.3 %copy-start.4 = (bf16[512,512]{1,0:T(8,128)(2,1)S(1)}, bf16[512,512]{1,0:T(8,128)(2,1)}, u32[]{:S(2)}) copy-start(bf16[512,512]{1,0:T(8,128)(2,1)} %vir_ref.1) | copy-start | bytes 1572868
  0.0 18.4 %copy-start.2 = (f32[512]{0:T(512)S(1)}, f32[512]{0:T(512)}, u32[]{:S(2)}) copy-start(f32[512]{0:T(512)} %param.15) | copy-start | bytes 6148
  0.0 18.4 %copy-start.3 = (f32[128]{0:T(128)S(1)}, f32[128]{0:T(128)}, u32[]{:S(2)}) copy-start(f32[128]{0:T(128)} %param.14) | copy-start | bytes 1540
  2.2 29.9 %all-to-all-start.2 = ((bf16[32,8,640]{2,1,0:T(8,128)(2,1)}), bf16[32,8,640]{2,1,0:T(8,128)(2,1)}, u32[]{:S(2)}, u32[]{:S(2)}) async-start(bf16[32,8,640]{2,1,0:T(8,128)(2,1)} %shard_map.91), calls=%async_computation.2 | async-start | bytes 655360 | tf_op jit(solution)/shard_map/all_to_all | solution.py:43
  19.2 7.0 %collective-permute-start.1 = (bf16[264,640]{1,0:T(8,128)(2,1)}, bf16[264,640]{1,0:T(8,128)(2,1)S(1)}, u32[]{:S(2)}, u32[]{:S(2)}) collective-permute-start(bf16[264,640]{1,0:T(8,128)(2,1)} %pad_maximum_fusion.1), channel_id=1, source_target_pairs={{0,1},{1,0},{2,3},{3,2},{4,5},{5,4},{6,7},{7,6},{8,9},{9,8},{10,11... | collective-permute-start | bytes 1013768 | tf_op jit(solution)/shard_map/ppermute | solution.py:221
  24.4 7.8 %copy-start.5 = (bf16[512,128]{1,0:T(8,128)(2,1)S(1)}, bf16[512,128]{1,0:T(8,128)(2,1)}, u32[]{:S(2)}) copy-start(bf16[512,128]{1,0:T(8,128)(2,1)} %occ_ref.1) | copy-start | bytes 393220
  33.4 3.1 %collective-permute-start = (bf16[32,640]{1,0:T(8,128)(2,1)S(1)}, bf16[32,640]{1,0:T(8,128)(2,1)S(1)}, u32[]{:S(2)}, u32[]{:S(2)}) collective-permute-start(bf16[32,640]{1,0:T(8,128)(2,1)S(1)} %convert_element_type.58), channel_id=1, source_target_pairs={{0,1},{1,0},{2,3},{3,2},{4,5},{5,4},{6,7},{7,6},{8,9},{9,8},{10,11... | collective-permute-start | bytes 122888 | tf_op jit(solution)/shard_map/ppermute | solution.py:221
  37.2 16.4 %copy-start.1 = (f32[16,384]{1,0:T(8,128)S(1)}, f32[16,384]{1,0:T(8,128)}, u32[]{:S(2)}) copy-start(f32[16,384]{1,0:T(8,128)} %constant.57.clone.down_ref) | copy-start | bytes 73732
  68.5 32.0 %copy-start = (f32[12,512]{1,0:T(8,128)S(1)}, f32[12,512]{1,0:T(8,128)}, u32[]{:S(2)}) copy-start(f32[12,512]{1,0:T(8,128)} %constant.58.clone.up_ref) | copy-start | bytes 73732

commit v7 on v6

--- a/solution.py
+++ b/solution.py
@@ -1,3 +1,5 @@
+import functools
+
 import jax
 import jax.numpy as jnp
 import numpy as np
@@ -18,6 +20,7 @@
 VMEM_LIMIT = 12 * 2**20
 YZ = ("yh", "z")
 ORB = ("x", "yl", "core")
+QUARTET = ("yl", "core")
 f32, f16, bf16 = jnp.float32, jnp.float16, jnp.bfloat16
 
 
@@ -99,45 +102,53 @@
         out_ref[k, :, no:] = vir
 
 
-def on_chip(body, shape, dtype, *args, scratch=(), last=False):
+def on_chip(body, shape, dtype, *args, scratch=(), last=False, count=0):
     space = pl.BlockSpec(memory_space=pltpu.VMEM)
+    out = jax.ShapeDtypeStruct(shape, dtype) if last else pltpu.VMEM(shape, dtype)
     return pl.pallas_call(
         body,
-        out_shape=jax.ShapeDtypeStruct(shape, dtype) if last else pltpu.VMEM(shape, dtype),
+        out_shape=(out,) * count if count else out,
         in_specs=[space] * len(args),
-        out_specs=space,
+        out_specs=(space,) * count if count else space,
         scratch_shapes=scratch,
         compiler_params=pltpu.CompilerParams(vmem_limit_bytes=VMEM_LIMIT),
     )(*[pltpu.with_memory_space_constraint(jnp.asarray(a), pltpu.VMEM) for a in args])
 
 
-def green_part(panel, occ_energy, vir_energy, occ, vir, scaled_ref):
-    no = occ.shape[1]
-    for energy, at in ((occ_energy, slice(0, no)), (vir_energy, slice(no, None))):
-        for t in range(NT):
-            decay = jnp.exp(-energy * MOMENTS[t])
-            scaled_ref[t * NC : (t + 1) * NC, at] = (panel[:, at] * decay).astype(bf16)
+def green_part(panel, energy, orbitals, scaled_ref, no):
+    for t in range(NT):
+        scaled_ref[t * NC : (t + 1) * NC, :] = (panel * jnp.exp(-energy * MOMENTS[t])).astype(bf16)
     flipped = (((1,), (1,)), ((), ()))
-    return (
-        lax.dot_general(occ, scaled_ref[:, :no], flipped, preferred_element_type=f32),
-        lax.dot_general(vir, scaled_ref[:, no:], flipped, preferred_element_type=f32),
-    )
-
-
-def green_body(panel_ref, other_panel_ref, occ_e_ref, vir_e_ref, other_e_ref, occ_ref, vir_ref, theirs_ref, out_ref, scaled_ref):
-    times, no = NT * NC, occ_ref.shape[1]
-    half = occ_ref.shape[0]
-    occ, vir = green_part(panel_ref[...], occ_e_ref[...], vir_e_ref[...], occ_ref[...], vir_ref[...], scaled_ref.at[0])
-    energy, theirs = other_e_ref[...], theirs_ref[:half]
-    other_occ, other_vir = green_part(
-        other_panel_ref[...].astype(f32),
-        energy[:, :no],
-        energy[:, no:],
-        theirs[:, :no],
-        theirs[:, no:],
-        scaled_ref.at[1],
-    )
-    occ, vir = occ + other_occ, vir + other_vir
+    occ = lax.dot_general(orbitals[:, :no], scaled_ref[:, :no], flipped, preferred_element_type=f32)
+    return occ, lax.dot_general(orbitals[:, no:], scaled_ref[:, no:], flipped, preferred_element_type=f32)
+
+
+def energy_of(rows):
+    return sum(rows[k : k + 1].astype(f32) for k in range(3))
+
+
+def offer_body(occ_ref, vir_ref, energy_ref, *out_refs):
+    me = lax.axis_index(QUARTET)
+    no = occ_ref.shape[1]
+    quarter = out_refs[0].shape[0] - 8
+    for k, out_ref in enumerate(out_refs):
+        rows = pl.ds(pl.multiple_of((me ^ k) * quarter, quarter), quarter)
+        out_ref[:quarter, :no] = occ_ref[rows, :]
+        out_ref[:quarter, no:] = vir_ref[rows, :]
+        out_ref[quarter:, :] = energy_ref[...]
+
+
+def green_body(no, panels_ref, *refs):
+    *theirs_refs, out_ref, scaled_ref = refs
+    me = lax.axis_index(QUARTET)
+    times = NT * NC
+    quarter = out_ref.shape[0]
+    occ, vir = 0.0, 0.0
+    for k, theirs_ref in enumerate(theirs_refs):
+        panel = panels_ref[me ^ k].astype(f32)
+        energy = energy_of(theirs_ref[quarter:, :])
+        one, two = green_part(panel, energy, theirs_ref[:quarter, :], scaled_ref.at[k], no)
+        occ, vir = occ + one, vir + two
     power = jnp.maximum(power_of(occ), power_of(vir))
     factor = jnp.exp2(-power)
     out_ref[:, :times] = occ * factor
@@ -217,49 +228,35 @@
     return jnp.stack([hi, mid, e - hi - mid]).astype(bf16)
 
 
-def to_other_core(x):
-    return lax.ppermute(x, "core", [(0, 1), (1, 0)])
-
-
 def local(panel_cols, occ_orbitals, vir_orbitals, occ_energy, vir_energy, coulomb):
     points, no = occ_orbitals.shape
-    half = points // 2
+    members = lax.axis_size(QUARTET)
+    quarter = points // members
     times = NT * NC
-    core = lax.axis_index("core")
-
-    def rows_of(x, k):
-        return jnp.where(k == 0, x[:half], x[half:])
 
     panel, picked = panel_rows(panel_cols, occ_orbitals, vir_orbitals)
+    width = panel.shape[1]
     occ_late, vir_late, _ = lax.optimization_barrier((occ_orbitals, vir_orbitals, picked))
-    coulomb = coulomb + 0.0 * picked[0, 0, 0].astype(f32)
-    panel, coulomb = lax.optimization_barrier((panel, coulomb))
-    energies = in_three(jnp.concatenate([occ_energy, vir_energy]))
-    theirs = jnp.concatenate([rows_of(occ_late, 1 - core), rows_of(vir_late, 1 - core)], axis=1)
-    theirs = jnp.concatenate([theirs, jnp.pad(energies, ((0, 5), (0, 0)))], axis=0)
-    theirs = to_other_core(theirs)
-    pieces = theirs[half : half + 3].astype(f32)
-    other_energy = pieces[0:1] + pieces[1:2] + pieces[2:3]
-    other_panel = to_other_core(panel.astype(bf16))
+    energies = jnp.pad(in_three(jnp.concatenate([occ_energy, vir_energy])), ((0, 5), (0, 0)))
+    mine, *others = on_chip(offer_body, (quarter + 8, width), bf16, occ_late, vir_late, energies, count=members)
+    theirs = [
+        lax.ppermute(x, QUARTET, [(i, i ^ k) for i in range(members)]) for k, x in enumerate(others, start=1)
+    ]
+    panel, *theirs = lax.optimization_barrier((panel, *theirs))
+    panels = moved(jnp.broadcast_to(panel.astype(bf16), (members, *panel.shape)), QUARTET)
     sent = on_chip(
-        green_body,
-        (half, 2 * times + 128),
+        functools.partial(green_body, no),
+        (quarter, 2 * times + 128),
         f32,
-        panel,
-        other_panel,
-        occ_energy.reshape(1, -1),
-        vir_energy.reshape(1, -1),
-        other_energy,
-        rows_of(occ_late, core),
-        rows_of(vir_late, core),
-        theirs,
-        scratch=[pltpu.VMEM((2, times, panel.shape[1]), bf16)],
+        panels,
+        mine,
+        *theirs,
+        scratch=[pltpu.VMEM((members, times, width), bf16)],
     ).astype(f16)
-    peers = lax.axis_size(("x", "yl"))
-    got = moved(sent.reshape(peers, half // peers, -1), ("x", "yl"))
+    got = moved(sent.reshape(lax.axis_size("x"), -1, 2 * times + 128), "x")
     table = [pltpu.VMEM((times, WIDTH), f32)]
     polar = on_chip(polar_body, (got.shape[1], WIDTH), f32, got.astype(f32), DOWN, scratch=table).astype(f16)
-    polar = moved(jnp.broadcast_to(polar, (lax.axis_size(ORB), *polar.shape)), ("core", "x", "yl"))
+    polar = moved(jnp.broadcast_to(polar, (lax.axis_size(ORB), *polar.shape)), (*QUARTET, "x"))
     polar = polar.reshape(points, WIDTH).astype(f32)
     part = on_chip(screen_body, (coulomb.shape[1], WIDTH), f32, coulomb, polar).astype(f16)
     blocks = moved(part.reshape(NC, -1, WIDTH), YZ).astype(f32)

time: 102 us -> 108 us (1.059)
  the two profiles are of different devices: /device:TPU:8 before, /device:TPU:64 now
where the time goes in v7:
time: 108 us; the launch traced here: 107 us
  blocking collectives  67.9 us (63%)
  starting transfers between devices  23 us (21%)
  Pallas kernels  7.32 us (7%)
  waiting for transfers between devices  6.13 us (6%)
  other arithmetic  1.34 us (1%)
    all_to_all x4, blocking collectives, moved(): return lax.all_to_all(x, axes, split_axis=0, concat_axis=0, tiled=True)  67.9 us
    all_to_all x1, starting transfers between devices, moved(): return lax.all_to_all(x, axes, split_axis=0, concat_axis=0, tiled=True)  15.4 us
    ppermute x3, starting transfers between devices, local(): lax.ppermute(x, QUARTET, [(i, i ^ k) for i in range(members)])  7.59 us
    all_to_all x1, waiting for transfers between devices, moved(): return lax.all_to_all(x, axes, split_axis=0, concat_axis=0, tiled=True)  6.12 us
    pallas_call x5, Pallas kernels, on_chip(): pl.pallas_call(body, out_shape=(out,) * count if count else out, in_specs...  5.1 us
    pallas_call x1, Pallas kernels, panel_rows(): pl.pallas_call(pick_body, out_shape=jax.ShapeDtypeStruct((blocks, SLOTS,...  2.23 us
  transfers between devices with their start and end apart: 4, of which 1 were waited for; matrix products, arithmetic and copies ran while one was open for 1% of the time, Pallas kernels for 0%

profile of v7, /device:TPU:64, one launch (start us, length us, event | category | flops | bytes accessed | tf_op | source)
XLA Modules:
  0.0 107.4 jit_solution(3822607282324289617)
XLA Ops:
  0.0 0.0 copy-start.5
  0.0 0.0 copy-start.7
  0.0 0.0 copy-start
  0.0 0.0 copy-start.2
  0.0 0.0 copy-start.6
  0.0 0.0 copy-start.8
  0.0 2.2 %shard_map.91 = bf16[32,8,640]{2,1,0:T(8,128)(2,1)} custom-call(s32[32]{0:T(128)} %cols_ref.1, bf16[512,128]{1,0:T(8,128)(2,1)} %occ_ref.2, bf16[512,512]{1,0:T(8,128)(2,1)} %vir_ref.2), custom_call_target="tpu_custom_call" | custom-call | tf_op jit(solution)/shard_map/pallas_call | solution.py:198
  2.3 15.4 %all-to-all-start.2 = ((bf16[32,8,640]{2,1,0:T(8,128)(2,1)}), bf16[32,8,640]{2,1,0:T(8,128)(2,1)S(1)}, u32[]{:S(2)}, u32[]{:S(2)}) async-start(bf16[32,8,640]{2,1,0:T(8,128)(2,1)} %shard_map.91), calls=%async_computation.2 | async-start | bytes 655360 | tf_op jit(solution)/shard_map/all_to_all | solution.py:46
  17.7 0.0 copy-done.6
  17.7 0.0 copy-done.8
  17.7 0.0 copy-done
  17.7 0.0 copy-done.2
  17.7 0.1 shard_map.92
  17.8 1.9 %collective-permute-start = (bf16[136,640]{1,0:T(8,128)(2,1)S(1)}, bf16[136,640]{1,0:T(8,128)(2,1)S(1)}, u32[]{:S(2)}, u32[]{:S(2)}) collective-permute-start(bf16[136,640]{1,0:T(8,128)(2,1)S(1)} %get-tuple-element.30), channel_id=1, source_target_pairs={{0,1},{1,0},{2,3},{3,2},{4,5},{5,4},{6,7},{7,6},{8,9},{9,8},{10,11... | collective-permute-start | bytes 522248 | tf_op jit(solution)/shard_map/ppermute | solution.py:243
  19.8 2.6 %collective-permute-start.1 = (bf16[136,640]{1,0:T(8,128)(2,1)S(1)}, bf16[136,640]{1,0:T(8,128)(2,1)S(1)}, u32[]{:S(2)}, u32[]{:S(2)}) collective-permute-start(bf16[136,640]{1,0:T(8,128)(2,1)S(1)} %get-tuple-element.31), channel_id=1, source_target_pairs={{0,2},{1,3},{2,0},{3,1},{4,6},{5,7},{6,4},{7,5},{8,10},{9,11},{10,... | collective-permute-start | bytes 522248 | tf_op jit(solution)/shard_map/ppermute | solution.py:243
  22.3 3.1 %collective-permute-start.2 = (bf16[136,640]{1,0:T(8,128)(2,1)S(1)}, bf16[136,640]{1,0:T(8,128)(2,1)S(1)}, u32[]{:S(2)}, u32[]{:S(2)}) collective-permute-start(bf16[136,640]{1,0:T(8,128)(2,1)S(1)} %get-tuple-element.32), channel_id=1, source_target_pairs={{0,3},{1,2},{2,1},{3,0},{4,7},{5,6},{6,5},{7,4},{8,11},{9,10},{10,... | collective-permute-start | bytes 522248 | tf_op jit(solution)/shard_map/ppermute | solution.py:243
  25.4 0.0 copy-done.7
  25.5 0.0 copy-done.5
  25.5 0.2 convert_reduce_fusion
  25.7 0.6 compare_reduce_fusion
  27.0 6.1 %all-to-all-done.2 = bf16[32,8,640]{2,1,0:T(8,128)(2,1)S(1)} async-done(((bf16[32,8,640]{2,1,0:T(8,128)(2,1)}), bf16[32,8,640]{2,1,0:T(8,128)(2,1)S(1)}, u32[]{:S(2)}, u32[]{:S(2)}) %all-to-all-start.2) | async-done | bytes 327712 | tf_op jit(solution)/shard_map/all_to_all | solution.py:46
  33.1 0.2 fusion.2
  33.3 0.0 collective-permute-done.refs_1_
  33.3 0.0 collective-permute-done.1.refs_2_
  33.3 0.0 collective-permute-done.2.refs_3_
  33.4 7.3 %all_to_all.35.panels_ref = bf16[4,32,640]{2,1,0:T(8,128)(2,1)S(1)} all-to-all(bf16[4,32,640]{2,1,0:T(8,128)(2,1)S(1)} %broadcast_in_dim.8), channel_id=1, replica_groups=mesh['yh'=4,'z'=8,'x'=4,'yl'=2,'core'=2] {'yl','core'}, dimensions={0} | all-to-all | bytes 327680 | tf_op jit(solution)/shard_map/all_to_all | solution.py:46
  40.7 0.0 copy-start.4
  40.7 1.2 %shard_map.93 = f32[128,1152]{1,0:T(8,128)S(1)} custom-call(bf16[4,32,640]{2,1,0:T(8,128)(2,1)S(1)} %all_to_all.35.panels_ref, bf16[136,640]{1,0:T(8,128)(2,1)S(1)} %get-tuple-element.34.refs_0_, bf16[136,640]{1,0:T(8,128)(2,1)S(1)} %collective-permute-done.refs_1_, bf16[136,640]{1,0:T(8,128)(2,1)S(1)} %collective-permute-done.1.refs_2_, ...), custom_call_target="tpu_custom_call" | custom-call | tf_op jit(solution)/shard_map/pallas_call | solution.py:108
  41.9 11.2 %all_to_all.36 = f16[4,32,1152]{2,1,0:T(8,128)(2,1)S(1)} all-to-all(f16[4,32,1152]{2,1,0:T(8,128)(2,1)S(1)} %bitcast.13), channel_id=1, replica_groups=mesh['yh'=4,'z'=8,'x'=4,'yl'=2,'core'=2] {'x'}, dimensions={0} | all-to-all | bytes 589824 | tf_op jit(solution)/shard_map/all_to_all | solution.py:46
  53.1 0.0 copy-done.4
  53.2 0.0 copy-start.1
  53.2 0.5 shard_map.94
  53.7 12.0 %all_to_all.37 = f16[16,32,384]{2,1,0:T(8,128)(2,1)S(1)} all-to-all(f16[16,32,384]{2,1,0:T(8,128)(2,1)S(1)} %broadcast_in_dim.14), channel_id=1, replica_groups=mesh['yh'=4,'z'=8,'x'=4,'yl'=2,'core'=2] {'yl','core','x'}, dimensions={0} | all-to-all | bytes 786432 | tf_op jit(solution)/shard_map/all_to_all | solution.py:46
  65.7 0.1 bitcast_convert_fusion.polar_ref
  65.8 0.0 copy-done.1
  65.8 2.2 %shard_map.95 = f32[1024,384]{1,0:T(8,128)S(1)} custom-call(f32[512,1024]{1,0:T(8,128)S(1)} %copy-done.1, f32[512,384]{1,0:T(8,128)S(1)} %bitcast_convert_fusion.polar_ref), custom_call_target="tpu_custom_call" | custom-call | tf_op jit(solution)/shard_map/pallas_call | solution.py:108
  68.1 0.1 convert_element_type.56
  68.2 37.3 %all_to_all.38 = f16[32,32,384]{2,1,0:T(8,128)(2,1)S(1)} all-to-all(f16[32,32,384]{2,1,0:T(8,128)(2,1)S(1)} %bitcast.12), channel_id=1, replica_groups=mesh['yh'=4,'z'=8,'x'=4,'yl'=2,'core'=2] {'yh','z'}, dimensions={0} | all-to-all | bytes 1572864 | tf_op jit(solution)/shard_map/all_to_all | solution.py:46
  105.5 0.0 copy-start.3
  105.5 0.2 convert_element_type.57.blocks_ref
  105.7 0.6 copy-done.3
  106.2 1.2 %shard_map.96 = f32[32,512]{1,0:T(8,128)} custom-call(f32[32,32,384]{2,1,0:T(8,128)S(1)} %convert_element_type.57.blocks_ref, f32[12,512]{1,0:T(8,128)S(1)} %copy-done.3), custom_call_target="tpu_custom_call" | custom-call | tf_op jit(solution)/shard_map/pallas_call | solution.py:108
  (10 shorter events, 0.2 us)
Async XLA Ops:
  0.0 25.5 %copy-start.5 = (pred[32,32]{1,0:T(32,128)(4,1)S(1)}, pred[32,32]{1,0:T(32,128)(4,1)}, u32[]{:S(2)}) copy-start(pred[32,32]{1,0:T(32,128)(4,1)} %constant.48.clone) | copy-start | bytes 3076
  0.0 25.4 %copy-start.7 = (s32[32]{0:T(128)S(1)}, s32[32]{0:T(128)}, u32[]{:S(2)}) copy-start(s32[32]{0:T(128)} %cols_ref.1) | copy-start | bytes 388
  0.0 17.7 %copy-start = (bf16[512,512]{1,0:T(8,128)(2,1)S(1)}, bf16[512,512]{1,0:T(8,128)(2,1)}, u32[]{:S(2)}) copy-start(bf16[512,512]{1,0:T(8,128)(2,1)} %vir_ref.2) | copy-start | bytes 1572868
  0.0 17.7 %copy-start.2 = (bf16[512,128]{1,0:T(8,128)(2,1)S(1)}, bf16[512,128]{1,0:T(8,128)(2,1)}, u32[]{:S(2)}) copy-start(bf16[512,128]{1,0:T(8,128)(2,1)} %occ_ref.2) | copy-start | bytes 393220
  0.0 17.6 %copy-start.6 = (f32[512]{0:T(512)S(1)}, f32[512]{0:T(512)}, u32[]{:S(2)}) copy-start(f32[512]{0:T(512)} %param.15) | copy-start | bytes 6148
  0.0 17.6 %copy-start.8 = (f32[128]{0:T(128)S(1)}, f32[128]{0:T(128)}, u32[]{:S(2)}) copy-start(f32[128]{0:T(128)} %param.14) | copy-start | bytes 1540
  2.3 30.8 %all-to-all-start.2 = ((bf16[32,8,640]{2,1,0:T(8,128)(2,1)}), bf16[32,8,640]{2,1,0:T(8,128)(2,1)S(1)}, u32[]{:S(2)}, u32[]{:S(2)}) async-start(bf16[32,8,640]{2,1,0:T(8,128)(2,1)} %shard_map.91), calls=%async_computation.2 | async-start | bytes 655360 | tf_op jit(solution)/shard_map/all_to_all | solution.py:46
  17.8 15.5 %collective-permute-start = (bf16[136,640]{1,0:T(8,128)(2,1)S(1)}, bf16[136,640]{1,0:T(8,128)(2,1)S(1)}, u32[]{:S(2)}, u32[]{:S(2)}) collective-permute-start(bf16[136,640]{1,0:T(8,128)(2,1)S(1)} %get-tuple-element.30), channel_id=1, source_target_pairs={{0,1},{1,0},{2,3},{3,2},{4,5},{5,4},{6,7},{7,6},{8,9},{9,8},{10,11... | collective-permute-start | bytes 522248 | tf_op jit(solution)/shard_map/ppermute | solution.py:243
  19.8 13.6 %collective-permute-start.1 = (bf16[136,640]{1,0:T(8,128)(2,1)S(1)}, bf16[136,640]{1,0:T(8,128)(2,1)S(1)}, u32[]{:S(2)}, u32[]{:S(2)}) collective-permute-start(bf16[136,640]{1,0:T(8,128)(2,1)S(1)} %get-tuple-element.31), channel_id=1, source_target_pairs={{0,2},{1,3},{2,0},{3,1},{4,6},{5,7},{6,4},{7,5},{8,10},{9,11},{10,... | collective-permute-start | bytes 522248 | tf_op jit(solution)/shard_map/ppermute | solution.py:243
  22.3 11.0 %collective-permute-start.2 = (bf16[136,640]{1,0:T(8,128)(2,1)S(1)}, bf16[136,640]{1,0:T(8,128)(2,1)S(1)}, u32[]{:S(2)}, u32[]{:S(2)}) collective-permute-start(bf16[136,640]{1,0:T(8,128)(2,1)S(1)} %get-tuple-element.32), channel_id=1, source_target_pairs={{0,3},{1,2},{2,1},{3,0},{4,7},{5,6},{6,5},{7,4},{8,11},{9,10},{10,... | collective-permute-start | bytes 522248 | tf_op jit(solution)/shard_map/ppermute | solution.py:243
  40.7 12.5 %copy-start.4 = (f32[16,384]{1,0:T(8,128)S(1)}, f32[16,384]{1,0:T(8,128)}, u32[]{:S(2)}) copy-start(f32[16,384]{1,0:T(8,128)} %constant.49.clone.down_ref) | copy-start | bytes 73732
  53.2 12.7 %copy-start.1 = (f32[512,1024]{1,0:T(8,128)S(1)}, f32[512,1024]{1,0:T(8,128)}, u32[]{:S(2)}) copy-start(f32[512,1024]{1,0:T(8,128)} %coulomb_ref.1) | copy-start | bytes 6291460
  105.5 0.8 copy-start.3

commit v8 on v6

--- a/solution.py
+++ b/solution.py
@@ -232,8 +232,6 @@
 
     panel, picked = panel_rows(panel_cols, occ_orbitals, vir_orbitals)
     occ_late, vir_late, _ = lax.optimization_barrier((occ_orbitals, vir_orbitals, picked))
-    coulomb = coulomb + 0.0 * picked[0, 0, 0].astype(f32)
-    panel, coulomb = lax.optimization_barrier((panel, coulomb))
     energies = in_three(jnp.concatenate([occ_energy, vir_energy]))
     theirs = jnp.concatenate([rows_of(occ_late, 1 - core), rows_of(vir_late, 1 - core)], axis=1)
     theirs = jnp.concatenate([theirs, jnp.pad(energies, ((0, 5), (0, 0)))], axis=0)

time: 102 us -> 101 us (level)
  waiting for transfers between devices: 7.1 us -> 12.2 us
  other arithmetic: 4.91 us -> 1.52 us
    all_to_all x1, waiting for transfers between devices: 5.92 us -> 11 us  [moved(): return lax.all_to_all(x, axes, split_axis=0, concat_axis=0, tiled=True)]
    add x1 -> x0, other arithmetic: 1.79 us -> none  [local(): coulomb = coulomb + 0.0 * picked[0, 0, 0].astype(f32)]
    slice x1 -> x0, local copies, waits for them, and re-layouts: 1.18 us -> none  [local(): coulomb = coulomb + 0.0 * picked[0, 0, 0].astype(f32)]
  transfers between devices with their start and end apart: 3 -> 3, of which waited for: 2 -> 3; matrix products, arithmetic and copies ran while one was open for 5% -> 1% of each run, Pallas kernels for 0% -> 0%
where the time goes in v8:
time: 101 us
  blocking collectives  59.1 us (59%)
  starting transfers between devices  19 us (19%)
  waiting for transfers between devices  12.2 us (12%)
  Pallas kernels  6.86 us (7%)
  other arithmetic  1.52 us (2%)
    all_to_all x3, blocking collectives, moved(): return lax.all_to_all(x, axes, split_axis=0, concat_axis=0, tiled=True)  59.1 us
    all_to_all x1, starting transfers between devices, moved(): return lax.all_to_all(x, axes, split_axis=0, concat_axis=0, tiled=True)  15.2 us
    all_to_all x1, waiting for transfers between devices, moved(): return lax.all_to_all(x, axes, split_axis=0, concat_axis=0, tiled=True)  11 us
    pallas_call x4, Pallas kernels, on_chip(): pl.pallas_call(body, out_shape=jax.ShapeDtypeStruct(shape, dtype) if last...  4.61 us
    ppermute x2, starting transfers between devices, to_other_core(): return lax.ppermute(x, 'core', [(0, 1), (1, 0)])  3.84 us
    pallas_call x1, Pallas kernels, panel_rows(): pl.pallas_call(pick_body, out_shape=jax.ShapeDtypeStruct((blocks, SLOTS,...  2.25 us
  transfers between devices with their start and end apart: 3, of which 3 were waited for; matrix products, arithmetic and copies ran while one was open for 1% of the time, Pallas kernels for 0%

profile of v8, /device:TPU:8, one launch (start us, length us, event | category | flops | bytes accessed | tf_op | source)
XLA Modules:
  0.0 100.6 jit_solution(8158370159549407704)
XLA Ops:
  0.0 0.0 copy-start.5
  0.0 0.0 copy-start.6
  0.0 0.0 copy-start.3
  0.0 0.0 copy-start.4
  0.0 2.3 %shard_map.91 = bf16[32,8,640]{2,1,0:T(8,128)(2,1)} custom-call(s32[32]{0:T(128)} %cols_ref.1, bf16[512,128]{1,0:T(8,128)(2,1)} %occ_ref.1, bf16[512,512]{1,0:T(8,128)(2,1)} %vir_ref.1), custom_call_target="tpu_custom_call" | custom-call | tf_op jit(solution)/shard_map/pallas_call | solution.py:187
  2.3 0.0 copy-start.8
  2.3 0.0 copy-start.7
  2.3 15.2 %all-to-all-start.2 = ((bf16[32,8,640]{2,1,0:T(8,128)(2,1)}), bf16[32,8,640]{2,1,0:T(8,128)(2,1)S(1)}, u32[]{:S(2)}, u32[]{:S(2)}) async-start(bf16[32,8,640]{2,1,0:T(8,128)(2,1)} %shard_map.91), calls=%async_computation.2 | async-start | bytes 655360 | tf_op jit(solution)/shard_map/all_to_all | solution.py:43
  17.5 0.0 copy-done.6
  17.5 0.0 copy-done.5
  17.6 0.0 copy-done.3
  17.6 0.0 copy-done.4
  17.7 1.9 %collective-permute-start.1 = (bf16[264,640]{1,0:T(8,128)(2,1)S(1)}, bf16[264,640]{1,0:T(8,128)(2,1)S(1)}, u32[]{:S(2)}, u32[]{:S(2)}) collective-permute-start(bf16[264,640]{1,0:T(8,128)(2,1)S(1)} %pad_maximum_fusion.1), channel_id=1, source_target_pairs={{0,1},{1,0},{2,3},{3,2},{4,5},{5,4},{6,7},{7,6},{8,9},{9,8},{10,11... | collective-permute-start | bytes 1013768 | tf_op jit(solution)/shard_map/ppermute | solution.py:221
  19.6 0.0 copy-done.8
  19.7 0.0 copy-done.7
  19.7 0.2 convert_reduce_fusion
  19.8 0.6 compare_reduce_fusion
  21.2 0.1 collective-permute-done.1.theirs_ref
  21.2 11.0 %all-to-all-done.2 = bf16[32,8,640]{2,1,0:T(8,128)(2,1)S(1)} async-done(((bf16[32,8,640]{2,1,0:T(8,128)(2,1)}), bf16[32,8,640]{2,1,0:T(8,128)(2,1)S(1)}, u32[]{:S(2)}, u32[]{:S(2)}) %all-to-all-start.2) | async-done | bytes 327712 | tf_op jit(solution)/shard_map/all_to_all | solution.py:43
  32.2 0.2 fusion.2
  32.4 1.9 %collective-permute-start = (bf16[32,640]{1,0:T(8,128)(2,1)S(1)}, bf16[32,640]{1,0:T(8,128)(2,1)S(1)}, u32[]{:S(2)}, u32[]{:S(2)}) collective-permute-start(bf16[32,640]{1,0:T(8,128)(2,1)S(1)} %convert_element_type.53), channel_id=1, source_target_pairs={{0,1},{1,0},{2,3},{3,2},{4,5},{5,4},{6,7},{7,6},{8,9},{9,8},{10,11... | collective-permute-start | bytes 122888 | tf_op jit(solution)/shard_map/ppermute | solution.py:221
  34.4 1.2 %collective-permute-done.other_panel_ref = bf16[32,640]{1,0:T(8,128)(2,1)S(1)} collective-permute-done((bf16[32,640]{1,0:T(8,128)(2,1)S(1)}, bf16[32,640]{1,0:T(8,128)(2,1)S(1)}, u32[]{:S(2)}, u32[]{:S(2)}) %collective-permute-start) | collective-permute-done | bytes 40992 | tf_op jit(solution)/shard_map/ppermute | solution.py:221
  35.6 0.7 shard_map.92
  36.3 0.1 convert_element_type.55
  36.4 0.0 copy-start.2
  36.4 16.2 %all_to_all.30 = f16[8,32,1152]{2,1,0:T(8,128)(2,1)S(1)} all-to-all(f16[8,32,1152]{2,1,0:T(8,128)(2,1)S(1)} %bitcast.17), channel_id=1, replica_groups=mesh['yh'=4,'z'=8,'x'=4,'yl'=2,'core'=2] {'x','yl'}, dimensions={0} | all-to-all | bytes 1179648 | tf_op jit(solution)/shard_map/all_to_all | solution.py:43
  52.6 0.1 convert_element_type.56.got_ref
  52.7 0.0 copy-done.2
  52.7 0.0 copy-start
  52.7 0.5 shard_map.93
  53.3 12.0 %all_to_all.31 = f16[16,32,384]{2,1,0:T(8,128)(2,1)S(1)} all-to-all(f16[16,32,384]{2,1,0:T(8,128)(2,1)S(1)} %broadcast_in_dim.4), channel_id=1, replica_groups=mesh['yh'=4,'z'=8,'x'=4,'yl'=2,'core'=2] {'core','x','yl'}, dimensions={0} | all-to-all | bytes 786432 | tf_op jit(solution)/shard_map/all_to_all | solution.py:43
  65.3 0.1 bitcast_convert_fusion.polar_ref
  65.4 0.0 copy-done
  65.4 2.2 %shard_map.94 = f32[1024,384]{1,0:T(8,128)S(1)} custom-call(f32[512,1024]{1,0:T(8,128)S(1)} %copy-done, f32[512,384]{1,0:T(8,128)S(1)} %bitcast_convert_fusion.polar_ref), custom_call_target="tpu_custom_call" | custom-call | tf_op jit(solution)/shard_map/pallas_call | solution.py:104
  67.6 0.1 convert_element_type.60
  67.7 30.9 %all_to_all.32 = f16[32,32,384]{2,1,0:T(8,128)(2,1)S(1)} all-to-all(f16[32,32,384]{2,1,0:T(8,128)(2,1)S(1)} %bitcast.16), channel_id=1, replica_groups=mesh['yh'=4,'z'=8,'x'=4,'yl'=2,'core'=2] {'yh','z'}, dimensions={0} | all-to-all | bytes 1572864 | tf_op jit(solution)/shard_map/all_to_all | solution.py:43
  98.6 0.0 copy-start.1
  98.6 0.2 convert_element_type.61.blocks_ref
  98.8 0.6 copy-done.1
  99.4 1.2 %shard_map.95 = f32[32,512]{1,0:T(8,128)} custom-call(f32[32,32,384]{2,1,0:T(8,128)S(1)} %convert_element_type.61.blocks_ref, f32[12,512]{1,0:T(8,128)S(1)} %copy-done.1), custom_call_target="tpu_custom_call" | custom-call | tf_op jit(solution)/shard_map/pallas_call | solution.py:104
  (13 shorter events, 0.2 us)
Async XLA Ops:
  0.0 17.5 %copy-start.5 = (bf16[512,512]{1,0:T(8,128)(2,1)S(1)}, bf16[512,512]{1,0:T(8,128)(2,1)}, u32[]{:S(2)}) copy-start(bf16[512,512]{1,0:T(8,128)(2,1)} %vir_ref.1) | copy-start | bytes 1572868
  0.0 17.5 %copy-start.6 = (bf16[512,128]{1,0:T(8,128)(2,1)S(1)}, bf16[512,128]{1,0:T(8,128)(2,1)}, u32[]{:S(2)}) copy-start(bf16[512,128]{1,0:T(8,128)(2,1)} %occ_ref.1) | copy-start | bytes 393220
  0.0 17.6 %copy-start.3 = (f32[512]{0:T(512)S(1)}, f32[512]{0:T(512)}, u32[]{:S(2)}) copy-start(f32[512]{0:T(512)} %param.15) | copy-start | bytes 6148
  0.0 17.6 %copy-start.4 = (f32[128]{0:T(128)S(1)}, f32[128]{0:T(128)}, u32[]{:S(2)}) copy-start(f32[128]{0:T(128)} %param.14) | copy-start | bytes 1540
  2.3 17.4 %copy-start.8 = (s32[32]{0:T(128)S(1)}, s32[32]{0:T(128)}, u32[]{:S(2)}) copy-start(s32[32]{0:T(128)} %cols_ref.1) | copy-start | bytes 388
  2.3 17.4 %copy-start.7 = (pred[32,32]{1,0:T(32,128)(4,1)S(1)}, pred[32,32]{1,0:T(32,128)(4,1)}, u32[]{:S(2)}) copy-start(pred[32,32]{1,0:T(32,128)(4,1)} %constant.53.clone) | copy-start | bytes 3076
  2.3 29.9 %all-to-all-start.2 = ((bf16[32,8,640]{2,1,0:T(8,128)(2,1)}), bf16[32,8,640]{2,1,0:T(8,128)(2,1)S(1)}, u32[]{:S(2)}, u32[]{:S(2)}) async-start(bf16[32,8,640]{2,1,0:T(8,128)(2,1)} %shard_map.91), calls=%async_computation.2 | async-start | bytes 655360 | tf_op jit(solution)/shard_map/all_to_all | solution.py:43
  17.7 3.5 %collective-permute-start.1 = (bf16[264,640]{1,0:T(8,128)(2,1)S(1)}, bf16[264,640]{1,0:T(8,128)(2,1)S(1)}, u32[]{:S(2)}, u32[]{:S(2)}) collective-permute-start(bf16[264,640]{1,0:T(8,128)(2,1)S(1)} %pad_maximum_fusion.1), channel_id=1, source_target_pairs={{0,1},{1,0},{2,3},{3,2},{4,5},{5,4},{6,7},{7,6},{8,9},{9,8},{10,11... | collective-permute-start | bytes 1013768 | tf_op jit(solution)/shard_map/ppermute | solution.py:221
  32.4 3.1 %collective-permute-start = (bf16[32,640]{1,0:T(8,128)(2,1)S(1)}, bf16[32,640]{1,0:T(8,128)(2,1)S(1)}, u32[]{:S(2)}, u32[]{:S(2)}) collective-permute-start(bf16[32,640]{1,0:T(8,128)(2,1)S(1)} %convert_element_type.53), channel_id=1, source_target_pairs={{0,1},{1,0},{2,3},{3,2},{4,5},{5,4},{6,7},{7,6},{8,9},{9,8},{10,11... | collective-permute-start | bytes 122888 | tf_op jit(solution)/shard_map/ppermute | solution.py:221
  36.4 16.3 %copy-start.2 = (f32[16,384]{1,0:T(8,128)S(1)}, f32[16,384]{1,0:T(8,128)}, u32[]{:S(2)}) copy-start(f32[16,384]{1,0:T(8,128)} %constant.54.clone.down_ref) | copy-start | bytes 73732
  52.7 12.7 %copy-start = (f32[512,1024]{1,0:T(8,128)S(1)}, f32[512,1024]{1,0:T(8,128)}, u32[]{:S(2)}) copy-start(f32[512,1024]{1,0:T(8,128)} %coulomb_ref.1) | copy-start | bytes 6291460
  98.6 0.8 copy-start.1

commit v9 on v7

--- a/solution.py
+++ b/solution.py
@@ -129,12 +129,14 @@
 
 def offer_body(occ_ref, vir_ref, energy_ref, *out_refs):
     me = lax.axis_index(QUARTET)
-    no = occ_ref.shape[1]
-    quarter = out_refs[0].shape[0] - 8
+    points, no = occ_ref.shape
+    quarter = points // len(out_refs)
+    run = quarter // lax.axis_size("x")
     for k, out_ref in enumerate(out_refs):
-        rows = pl.ds(pl.multiple_of((me ^ k) * quarter, quarter), quarter)
-        out_ref[:quarter, :no] = occ_ref[rows, :]
-        out_ref[:quarter, no:] = vir_ref[rows, :]
+        for x in range(quarter // run):
+            rows = pl.ds(pl.multiple_of(x * quarter + (me ^ k) * run, run), run)
+            out_ref[x * run : (x + 1) * run, :no] = occ_ref[rows, :]
+            out_ref[x * run : (x + 1) * run, no:] = vir_ref[rows, :]
         out_ref[quarter:, :] = energy_ref[...]
 
 
@@ -256,7 +258,7 @@
     got = moved(sent.reshape(lax.axis_size("x"), -1, 2 * times + 128), "x")
     table = [pltpu.VMEM((times, WIDTH), f32)]
     polar = on_chip(polar_body, (got.shape[1], WIDTH), f32, got.astype(f32), DOWN, scratch=table).astype(f16)
-    polar = moved(jnp.broadcast_to(polar, (lax.axis_size(ORB), *polar.shape)), (*QUARTET, "x"))
+    polar = moved(jnp.broadcast_to(polar, (lax.axis_size(ORB), *polar.shape)), ORB)
     polar = polar.reshape(points, WIDTH).astype(f32)
     part = on_chip(screen_body, (coulomb.shape[1], WIDTH), f32, coulomb, polar).astype(f16)
     blocks = moved(part.reshape(NC, -1, WIDTH), YZ).astype(f32)

time: 108 us -> 108 us (level)
  the two profiles are of different devices: /device:TPU:64 before, /device:TPU:8 now
where the time goes in v9:
time: 108 us
  blocking collectives  68.5 us (63%)
  starting transfers between devices  22.7 us (21%)
  Pallas kernels  7.32 us (7%)
  waiting for transfers between devices  6.4 us (6%)
  other arithmetic  1.34 us (1%)
    all_to_all x4, blocking collectives, moved(): return lax.all_to_all(x, axes, split_axis=0, concat_axis=0, tiled=True)  68.5 us
    all_to_all x1, starting transfers between devices, moved(): return lax.all_to_all(x, axes, split_axis=0, concat_axis=0, tiled=True)  15.1 us
    ppermute x3, starting transfers between devices, local(): lax.ppermute(x, QUARTET, [(i, i ^ k) for i in range(members)])  7.59 us
    all_to_all x1, waiting for transfers between devices, moved(): return lax.all_to_all(x, axes, split_axis=0, concat_axis=0, tiled=True)  5.43 us
    pallas_call x5, Pallas kernels, on_chip(): pl.pallas_call(body, out_shape=(out,) * count if count else out, in_specs...  5.1 us
    pallas_call x1, Pallas kernels, panel_rows(): pl.pallas_call(pick_body, out_shape=jax.ShapeDtypeStruct((blocks, SLOTS,...  2.23 us
  transfers between devices with their start and end apart: 4, of which 2 were waited for; matrix products, arithmetic and copies ran while one was open for 1% of the time, Pallas kernels for 0%

profile of v9, /device:TPU:8, one launch (start us, length us, event | category | flops | bytes accessed | tf_op | source)
XLA Modules:
  0.0 108.0 jit_solution(7582919449801028270)
XLA Ops:
  0.0 0.0 copy-start.5
  0.0 0.0 copy-start.7
  0.0 0.0 copy-start
  0.0 0.0 copy-start.2
  0.0 0.0 copy-start.6
  0.0 0.0 copy-start.8
  0.0 2.2 %shard_map.91 = bf16[32,8,640]{2,1,0:T(8,128)(2,1)} custom-call(s32[32]{0:T(128)} %cols_ref.1, bf16[512,128]{1,0:T(8,128)(2,1)} %occ_ref.2, bf16[512,512]{1,0:T(8,128)(2,1)} %vir_ref.2), custom_call_target="tpu_custom_call" | custom-call | tf_op jit(solution)/shard_map/pallas_call | solution.py:200
  2.3 15.1 %all-to-all-start.2 = ((bf16[32,8,640]{2,1,0:T(8,128)(2,1)}), bf16[32,8,640]{2,1,0:T(8,128)(2,1)S(1)}, u32[]{:S(2)}, u32[]{:S(2)}) async-start(bf16[32,8,640]{2,1,0:T(8,128)(2,1)} %shard_map.91), calls=%async_computation.2 | async-start | bytes 655360 | tf_op jit(solution)/shard_map/all_to_all | solution.py:46
  17.3 0.0 copy-done.6
  17.4 0.0 copy-done.8
  17.4 0.0 copy-done
  17.4 0.0 copy-done.2
  17.4 0.1 shard_map.92
  17.5 1.9 %collective-permute-start = (bf16[136,640]{1,0:T(8,128)(2,1)S(1)}, bf16[136,640]{1,0:T(8,128)(2,1)S(1)}, u32[]{:S(2)}, u32[]{:S(2)}) collective-permute-start(bf16[136,640]{1,0:T(8,128)(2,1)S(1)} %get-tuple-element.30), channel_id=1, source_target_pairs={{0,1},{1,0},{2,3},{3,2},{4,5},{5,4},{6,7},{7,6},{8,9},{9,8},{10,11... | collective-permute-start | bytes 522248 | tf_op jit(solution)/shard_map/ppermute | solution.py:245
  19.4 3.3 %collective-permute-start.1 = (bf16[136,640]{1,0:T(8,128)(2,1)S(1)}, bf16[136,640]{1,0:T(8,128)(2,1)S(1)}, u32[]{:S(2)}, u32[]{:S(2)}) collective-permute-start(bf16[136,640]{1,0:T(8,128)(2,1)S(1)} %get-tuple-element.31), channel_id=1, source_target_pairs={{0,2},{1,3},{2,0},{3,1},{4,6},{5,7},{6,4},{7,5},{8,10},{9,11},{10,... | collective-permute-start | bytes 522248 | tf_op jit(solution)/shard_map/ppermute | solution.py:245
  22.7 2.4 %collective-permute-start.2 = (bf16[136,640]{1,0:T(8,128)(2,1)S(1)}, bf16[136,640]{1,0:T(8,128)(2,1)S(1)}, u32[]{:S(2)}, u32[]{:S(2)}) collective-permute-start(bf16[136,640]{1,0:T(8,128)(2,1)S(1)} %get-tuple-element.32), channel_id=1, source_target_pairs={{0,3},{1,2},{2,1},{3,0},{4,7},{5,6},{6,5},{7,4},{8,11},{9,10},{10,... | collective-permute-start | bytes 522248 | tf_op jit(solution)/shard_map/ppermute | solution.py:245
  25.1 0.0 copy-done.7
  25.1 0.0 copy-done.5
  25.2 0.2 convert_reduce_fusion
  25.3 0.6 compare_reduce_fusion
  26.6 5.4 %all-to-all-done.2 = bf16[32,8,640]{2,1,0:T(8,128)(2,1)S(1)} async-done(((bf16[32,8,640]{2,1,0:T(8,128)(2,1)}), bf16[32,8,640]{2,1,0:T(8,128)(2,1)S(1)}, u32[]{:S(2)}, u32[]{:S(2)}) %all-to-all-start.2) | async-done | bytes 327712 | tf_op jit(solution)/shard_map/all_to_all | solution.py:46
  32.1 0.2 fusion.2
  32.3 0.0 collective-permute-done.refs_1_
  32.3 0.0 collective-permute-done.1.refs_2_
  32.3 1.0 collective-permute-done.2.refs_3_
  33.3 6.9 %all_to_all.35.panels_ref = bf16[4,32,640]{2,1,0:T(8,128)(2,1)S(1)} all-to-all(bf16[4,32,640]{2,1,0:T(8,128)(2,1)S(1)} %broadcast_in_dim.8), channel_id=1, replica_groups=mesh['yh'=4,'z'=8,'x'=4,'yl'=2,'core'=2] {'yl','core'}, dimensions={0} | all-to-all | bytes 327680 | tf_op jit(solution)/shard_map/all_to_all | solution.py:46
  40.2 0.0 copy-start.4
  40.2 1.2 %shard_map.93 = f32[128,1152]{1,0:T(8,128)S(1)} custom-call(bf16[4,32,640]{2,1,0:T(8,128)(2,1)S(1)} %all_to_all.35.panels_ref, bf16[136,640]{1,0:T(8,128)(2,1)S(1)} %get-tuple-element.34.refs_0_, bf16[136,640]{1,0:T(8,128)(2,1)S(1)} %collective-permute-done.refs_1_, bf16[136,640]{1,0:T(8,128)(2,1)S(1)} %collective-permute-done.1.refs_2_, ...), custom_call_target="tpu_custom_call" | custom-call | tf_op jit(solution)/shard_map/pallas_call | solution.py:108
  41.5 11.2 %all_to_all.36 = f16[4,32,1152]{2,1,0:T(8,128)(2,1)S(1)} all-to-all(f16[4,32,1152]{2,1,0:T(8,128)(2,1)S(1)} %bitcast.13), channel_id=1, replica_groups=mesh['yh'=4,'z'=8,'x'=4,'yl'=2,'core'=2] {'x'}, dimensions={0} | all-to-all | bytes 589824 | tf_op jit(solution)/shard_map/all_to_all | solution.py:46
  52.7 0.0 copy-done.4
  52.7 0.0 copy-start.1
  52.7 0.5 shard_map.94
  53.3 12.5 %all_to_all.37 = f16[16,32,384]{2,1,0:T(8,128)(2,1)S(1)} all-to-all(f16[16,32,384]{2,1,0:T(8,128)(2,1)S(1)} %broadcast_in_dim.14), channel_id=1, replica_groups=mesh['yh'=4,'z'=8,'x'=4,'yl'=2,'core'=2] {'x','yl','core'}, dimensions={0} | all-to-all | bytes 786432 | tf_op jit(solution)/shard_map/all_to_all | solution.py:46
  65.8 0.1 bitcast_convert_fusion.polar_ref
  65.9 0.0 copy-done.1
  65.9 2.2 %shard_map.95 = f32[1024,384]{1,0:T(8,128)S(1)} custom-call(f32[512,1024]{1,0:T(8,128)S(1)} %copy-done.1, f32[512,384]{1,0:T(8,128)S(1)} %bitcast_convert_fusion.polar_ref), custom_call_target="tpu_custom_call" | custom-call | tf_op jit(solution)/shard_map/pallas_call | solution.py:108
  68.1 0.1 convert_element_type.56
  68.3 37.8 %all_to_all.38 = f16[32,32,384]{2,1,0:T(8,128)(2,1)S(1)} all-to-all(f16[32,32,384]{2,1,0:T(8,128)(2,1)S(1)} %bitcast.12), channel_id=1, replica_groups=mesh['yh'=4,'z'=8,'x'=4,'yl'=2,'core'=2] {'yh','z'}, dimensions={0} | all-to-all | bytes 1572864 | tf_op jit(solution)/shard_map/all_to_all | solution.py:46
  106.0 0.0 copy-start.3
  106.0 0.2 convert_element_type.57.blocks_ref
  106.2 0.6 copy-done.3
  106.8 1.2 %shard_map.96 = f32[32,512]{1,0:T(8,128)} custom-call(f32[32,32,384]{2,1,0:T(8,128)S(1)} %convert_element_type.57.blocks_ref, f32[12,512]{1,0:T(8,128)S(1)} %copy-done.3), custom_call_target="tpu_custom_call" | custom-call | tf_op jit(solution)/shard_map/pallas_call | solution.py:108
  (10 shorter events, 0.2 us)
Async XLA Ops:
  0.0 25.1 %copy-start.5 = (pred[32,32]{1,0:T(32,128)(4,1)S(1)}, pred[32,32]{1,0:T(32,128)(4,1)}, u32[]{:S(2)}) copy-start(pred[32,32]{1,0:T(32,128)(4,1)} %constant.48.clone) | copy-start | bytes 3076
  0.0 25.1 %copy-start.7 = (s32[32]{0:T(128)S(1)}, s32[32]{0:T(128)}, u32[]{:S(2)}) copy-start(s32[32]{0:T(128)} %cols_ref.1) | copy-start | bytes 388
  0.0 17.4 %copy-start = (bf16[512,512]{1,0:T(8,128)(2,1)S(1)}, bf16[512,512]{1,0:T(8,128)(2,1)}, u32[]{:S(2)}) copy-start(bf16[512,512]{1,0:T(8,128)(2,1)} %vir_ref.2) | copy-start | bytes 1572868
  0.0 17.4 %copy-start.2 = (bf16[512,128]{1,0:T(8,128)(2,1)S(1)}, bf16[512,128]{1,0:T(8,128)(2,1)}, u32[]{:S(2)}) copy-start(bf16[512,128]{1,0:T(8,128)(2,1)} %occ_ref.2) | copy-start | bytes 393220
  0.0 17.3 %copy-start.6 = (f32[512]{0:T(512)S(1)}, f32[512]{0:T(512)}, u32[]{:S(2)}) copy-start(f32[512]{0:T(512)} %param.15) | copy-start | bytes 6148
  0.0 17.3 %copy-start.8 = (f32[128]{0:T(128)S(1)}, f32[128]{0:T(128)}, u32[]{:S(2)}) copy-start(f32[128]{0:T(128)} %param.14) | copy-start | bytes 1540
  2.3 29.8 %all-to-all-start.2 = ((bf16[32,8,640]{2,1,0:T(8,128)(2,1)}), bf16[32,8,640]{2,1,0:T(8,128)(2,1)S(1)}, u32[]{:S(2)}, u32[]{:S(2)}) async-start(bf16[32,8,640]{2,1,0:T(8,128)(2,1)} %shard_map.91), calls=%async_computation.2 | async-start | bytes 655360 | tf_op jit(solution)/shard_map/all_to_all | solution.py:46
  17.5 14.8 %collective-permute-start = (bf16[136,640]{1,0:T(8,128)(2,1)S(1)}, bf16[136,640]{1,0:T(8,128)(2,1)S(1)}, u32[]{:S(2)}, u32[]{:S(2)}) collective-permute-start(bf16[136,640]{1,0:T(8,128)(2,1)S(1)} %get-tuple-element.30), channel_id=1, source_target_pairs={{0,1},{1,0},{2,3},{3,2},{4,5},{5,4},{6,7},{7,6},{8,9},{9,8},{10,11... | collective-permute-start | bytes 522248 | tf_op jit(solution)/shard_map/ppermute | solution.py:245
  19.4 12.9 %collective-permute-start.1 = (bf16[136,640]{1,0:T(8,128)(2,1)S(1)}, bf16[136,640]{1,0:T(8,128)(2,1)S(1)}, u32[]{:S(2)}, u32[]{:S(2)}) collective-permute-start(bf16[136,640]{1,0:T(8,128)(2,1)S(1)} %get-tuple-element.31), channel_id=1, source_target_pairs={{0,2},{1,3},{2,0},{3,1},{4,6},{5,7},{6,4},{7,5},{8,10},{9,11},{10,... | collective-permute-start | bytes 522248 | tf_op jit(solution)/shard_map/ppermute | solution.py:245
  22.7 10.6 %collective-permute-start.2 = (bf16[136,640]{1,0:T(8,128)(2,1)S(1)}, bf16[136,640]{1,0:T(8,128)(2,1)S(1)}, u32[]{:S(2)}, u32[]{:S(2)}) collective-permute-start(bf16[136,640]{1,0:T(8,128)(2,1)S(1)} %get-tuple-element.32), channel_id=1, source_target_pairs={{0,3},{1,2},{2,1},{3,0},{4,7},{5,6},{6,5},{7,4},{8,11},{9,10},{10,... | collective-permute-start | bytes 522248 | tf_op jit(solution)/shard_map/ppermute | solution.py:245
  40.2 12.5 %copy-start.4 = (f32[16,384]{1,0:T(8,128)S(1)}, f32[16,384]{1,0:T(8,128)}, u32[]{:S(2)}) copy-start(f32[16,384]{1,0:T(8,128)} %constant.49.clone.down_ref) | copy-start | bytes 73732
  52.7 13.2 %copy-start.1 = (f32[512,1024]{1,0:T(8,128)S(1)}, f32[512,1024]{1,0:T(8,128)}, u32[]{:S(2)}) copy-start(f32[512,1024]{1,0:T(8,128)} %coulomb_ref.1) | copy-start | bytes 6291460
  106.0 0.8 copy-start.3
